TPU v7x, 32 devices: a whole 2x2x4 slice. The times are simulated.
32 devices in a mesh: gx: 4 (over y, x), gy: 4 (over z), gz: 2 (over core).
Axes of the slice: x: 2, y: 2, z: 4, core: 2. Of those that a mesh axis runs over, the one named last changes fastest.
Arguments:
- membrane: float32 [64, 64, 512], P('gx', 'gy', 'gz'), may hold values from 0 to 0.95
- recovery: float32 [64, 64, 512], P('gx', 'gy', 'gz'), may hold values from 0 to 2
- extracellular: float32 [64, 64, 512], P('gx', 'gy', 'gz'), may hold values from -6 to 6
- fiber_scale: float32 [64, 64, 512], P('gx', 'gy', 'gz'), may hold values from 0.5 to 2
- labels: int32 [8, 8, 64], P('gx', 'gy', 'gz'), may hold values from 0 to 2
Outputs:
- membrane_next: float32 [64, 64, 512], P('gx', 'gy', 'gz')
- recovery_next: float32 [64, 64, 512], P('gx', 'gy', 'gz')
- extracellular_next: float32 [64, 64, 512], P('gx', 'gy', 'gz')
All inputs are finite; a program needn't handle non-finite values.
Results may differ from a plain program's by a relative error of at most 0.0003.
Values sent between devices are 32-bit elements; how exact they have to be, the bound alone decides.
A program may use at most 128 MiB of HBM per device.

v0:
```python
import functools

import jax
import jax.numpy as jnp
from jax import lax
from jax.experimental import pallas as pl
from jax.experimental.pallas import tpu as pltpu
from jax.sharding import PartitionSpec as P

COARSE_SWEEPS = 8
TIME_STEP = 0.05
ionic_gain = 8.0
ionic_onset = 0.15
recovery_rate = 0.01
MESH = pl.DeviceIdType.MESH
LANES = 128
F32 = jnp.float32

INNER, U, OUTER, V, NEXT, RED, BLACK, FIXED, LAST = range(9)
INNER1, OUTER1, RED1, BLACK1, FIXED1, LASTRED1, LASTBLACK1 = range(7)
EXCHANGES = (
    (0, INNER, 2),
    (0, OUTER, 2),
    (1, INNER1, 2),
    (0, NEXT, 1),
    (0, RED, 1),
    (0, BLACK, 1),
    (1, RED1, 1),
    (1, BLACK1, 1),
    (1, LASTRED1, 1),
    (1, LASTBLACK1, 1),
    (0, LAST, 1),
)
SIDES = 5


def dot(a, b):
    return jnp.dot(a, b, precision=lax.Precision.HIGHEST, preferred_element_type=F32)


def pair_matrix(rows, cols, offset):
    j = lax.broadcasted_iota(jnp.int32, (rows, cols), 0)
    k = lax.broadcasted_iota(jnp.int32, (rows, cols), 1)
    return jnp.where(lax.shift_right_logical(j, 1) + offset == k, 1.0, 0.0).astype(F32)


def copy_matrix(rows, cols, shift):
    k = lax.broadcasted_iota(jnp.int32, (rows, cols), 0)
    j = lax.broadcasted_iota(jnp.int32, (rows, cols), 1)
    return jnp.where(lax.shift_right_logical(j, shift) == k, 1.0, 0.0).astype(F32)


class Grid:
    def __init__(self, planes, rows, lanes):
        self.planes, self.rows, self.lanes = planes, rows, lanes
        self.row = lax.broadcasted_iota(jnp.int32, (rows, lanes), 0)
        self.lane = lax.broadcasted_iota(jnp.int32, (rows, lanes), 1)
        self.even = jnp.bitwise_and(self.row + self.lane, 1) == 0
        self.odd = jnp.bitwise_and(self.row + self.lane, 1) == 1

    def colour(self, x, colour):
        return self.even if (x + colour) % 2 == 0 else self.odd


class Halo:
    def __init__(self, grid, refs, iz):
        self.grid, self.iz = grid, iz
        self.xs, self.ys, self.zs, self.xh, self.yh, self.zh = refs
        self.flane = lax.broadcasted_iota(jnp.int32, (grid.rows, LANES), 1)

    def faces(self, slot, planes):
        g = self.grid
        acc = jnp.zeros((g.rows, LANES), F32)
        for x, val in planes:
            self.ys[0, slot, x : x + 1, :] = val[0:1]
            self.ys[1, slot, x : x + 1, :] = val[g.rows - 1 :]
            if g.lanes > LANES:
                end = jnp.where(self.iz == 0, val[:, g.lanes - LANES :], val[:, :LANES])
            else:
                end = val
            acc = jnp.where(self.flane == x, pltpu.roll(end, x + 1 - self.iz, 1), acc)
            yield
        self.zs[slot] = acc

    def put_ends(self, slot, ref):
        self.xs[0, slot] = ref[0]
        self.xs[1, slot] = ref[self.grid.planes - 1]

    def put_rest(self, slot, ref):
        for _ in self.faces(slot, [(x, ref[x]) for x in range(self.grid.planes)]):
            pass

    def put(self, slot, ref):
        self.put_ends(slot, ref)
        self.put_rest(slot, ref)

    def neighbours(self, slot, planes, x, edge=False):
        g = self.grid
        val = planes(x)
        xm = planes(x - 1) if x > 0 else self.xh[0, slot]
        xp = planes(x + 1) if x < g.planes - 1 else self.xh[1, slot]
        shape = (g.rows, g.lanes)
        low = jnp.broadcast_to(self.yh[0, slot, x : x + 1, :], shape)
        high = jnp.broadcast_to(self.yh[1, slot, x : x + 1, :], shape)
        ym = jnp.where(g.row == 0, low, pltpu.roll(val, 1, 0))
        yp = jnp.where(g.row == g.rows - 1, high, pltpu.roll(val, g.rows - 1, 0))
        side = jnp.broadcast_to(self.zh[slot, :, x : x + 1], shape)
        side_m, side_p = side, side
        if edge:
            side_m = jnp.where(self.iz == 0, 0.0, side)
            side_p = jnp.where(self.iz == 0, side, 0.0)
        zm = jnp.where(g.lane == 0, side_m, pltpu.roll(val, 1, 1))
        zp = jnp.where(g.lane == g.lanes - 1, side_p, pltpu.roll(val, g.lanes - 1, 1))
        return val, (xm, xp, ym, yp, zm, zp)


def halve_rows(tmp, slot, val):
    rows, lanes = val.shape
    parts = []
    for k in range(lanes // LANES):
        at = 2 * slot + k
        tmp[at, 0:rows, :] = val[:, k * LANES : (k + 1) * LANES]
        parts.append(tmp[at, pl.ds(0, rows // 2, 2), :] + tmp[at, pl.ds(1, rows // 2, 2), :])
    return parts[0] if len(parts) == 1 else jnp.concatenate(parts, axis=1)


def double_rows(tmp, slot, val):
    rows, lanes = val.shape
    parts = []
    for k in range(lanes // LANES):
        at = 2 * slot + k
        piece = val[:, k * LANES : (k + 1) * LANES]
        tmp[at, pl.ds(0, rows, 2), :] = piece
        tmp[at, pl.ds(1, rows, 2), :] = piece
        parts.append(tmp[at, 0 : 2 * rows, :])
    return parts[0] if len(parts) == 1 else jnp.concatenate(parts, axis=1)


def kernel(counts, *refs):
    (mem, rec, ext, fib, lab, mem_out, ext_out) = refs[:7]
    (xs0, ys0, zs0, xh0, yh0, zh0, xs1, ys1, zs1, xh1, yh1, zh1) = refs[7:19]
    (in0, out0, uu, w0, c0, d0, b0, va, vb, tmp, tall) = refs[19:30]
    (in1, out1, c1, d1, b1, v1a, v1b) = refs[30:37]
    (gc_own, gc, gr_own, gr, in2, out2, c2, d2, b2, v2a, v2b) = refs[37:48]
    (c3, b3, v3, k3, h3, send_sem, recv_sem, gs_sem, gr_sem) = refs[48:]
    nx, ny, nz = counts
    ix, iy, iz = lax.axis_index("gx"), lax.axis_index("gy"), lax.axis_index("gz")
    me = (ix * ny + iy) * nz + iz
    total = nx * ny * nz

    for ref in (xh0, yh0, xh1, yh1):
        ref[...] = jnp.zeros(ref.shape, F32)

    barrier = pltpu.get_barrier_semaphore()

    def others(body):
        def step(i, carry):
            dev = lax.rem(me + i, total)
            body(dev, (dev // (ny * nz), lax.rem(dev // nz, ny), lax.rem(dev, nz)))
            return carry

        lax.fori_loop(1, total, step, 0)

    others(lambda dev, where: pl.semaphore_signal(barrier, inc=1, device_id=where, device_id_type=MESH))

    g0 = Grid(*mem.shape)
    g1 = Grid(*in1.shape)
    halo0 = Halo(g0, (xs0, ys0, zs0, xh0, yh0, zh0), iz)
    halo1 = Halo(g1, (xs1, ys1, zs1, xh1, yh1, zh1), iz)

    def copies(number):
        level, first, slots = EXCHANGES[number]
        h = (halo0, halo1)[level]
        part = pl.ds(first, slots)
        plan = (
            (h.xs.at[0, part], h.xh.at[1, part], (ix - 1, iy, iz), ix > 0, ix < nx - 1),
            (h.xs.at[1, part], h.xh.at[0, part], (ix + 1, iy, iz), ix < nx - 1, ix > 0),
            (h.ys.at[0, part], h.yh.at[1, part], (ix, iy - 1, iz), iy > 0, iy < ny - 1),
            (h.ys.at[1, part], h.yh.at[0, part], (ix, iy + 1, iz), iy < ny - 1, iy > 0),
            (h.zs.at[part], h.zh.at[part], (ix, iy, 1 - iz), None, None),
        )
        for side, (src, dst, dev, goes, comes) in enumerate(plan):
            copy = pltpu.make_async_remote_copy(
                src_ref=src,
                dst_ref=dst,
                send_sem=send_sem.at[number * SIDES + side],
                recv_sem=recv_sem.at[number * SIDES + side],
                device_id=dev,
                device_id_type=MESH,
            )
            yield copy, goes, comes

    ends, rest = slice(0, 2), slice(2, SIDES)

    def send(number, sides=slice(0, SIDES)):
        for copy, goes, _ in list(copies(number))[sides]:
            if goes is None:
                copy.start()
            else:
                pl.when(goes)(copy.start)

    def arrive(number, sides=slice(0, SIDES)):
        for copy, _, comes in list(copies(number))[sides]:
            if comes is None:
                copy.wait_recv()
            else:
                pl.when(comes)(copy.wait_recv)

    def inner_first(number, count):
        arrive(number, rest)
        yield from range(1, count - 1)
        arrive(number, ends)
        yield 0
        yield count - 1

    def publish(number, halo, slot, ref):
        halo.put_ends(slot, ref)
        send(number, ends)
        halo.put_rest(slot, ref)
        send(number, rest)

    def sent(number):
        for copy, goes, _ in copies(number):
            if goes is None:
                copy.wait_send()
            else:
                pl.when(goes)(copy.wait_send)

    def gather_send(own, whole, which):
        def go(dev, where):
            pltpu.make_async_remote_copy(
                src_ref=own,
                dst_ref=whole.at[me],
                send_sem=gs_sem.at[which],
                recv_sem=gr_sem.at[which],
                device_id=where,
                device_id_type=MESH,
            ).start()

        others(go)
        whole[pl.ds(me, 1)] = own[...][None]

    def gather_wait(whole, which, recv):
        rest = whole.at[pl.ds(0, total - 1)]
        copy = pltpu.make_async_remote_copy(
            src_ref=rest,
            dst_ref=rest,
            send_sem=gs_sem.at[which],
            recv_sem=gr_sem.at[which],
            device_id=(ix, iy, 1 - iz),
            device_id_type=MESH,
        )
        if recv:
            copy.wait_recv()
        else:
            copy.wait_send()

    X0, R0, Z0 = mem.shape
    X1, R1, Z1 = in1.shape
    X2 = X1 // 2
    R2 = R1 // 2
    half = Z1 // 2

    widen8 = copy_matrix(lab.shape[2], Z0, 3)
    lab_planes = []
    for bx in range(lab.shape[0]):
        wide = jnp.dot(lab[bx].astype(F32), widen8, preferred_element_type=F32)
        lab_planes.append(
            jnp.concatenate(
                [jnp.broadcast_to(wide[by : by + 1], (8, Z0)) for by in range(lab.shape[1])], axis=0
            )
        )

    def label_of(x):
        return lab_planes[x // 8]

    for x in range(X0):
        label = label_of(x)
        in0[x] = jnp.where(label == 1.0, 1.0, jnp.where(label == 2.0, 0.3, 0.0)) * fib[x]
        out0[x] = jnp.where(label == 0.0, 3.0, 1.0)
        uu[x] = mem[x] + ext[x]
    halo0.put(INNER, in0)
    halo0.put(U, uu)
    pl.semaphore_wait(barrier, total - 1)
    send(0)
    halo0.put(OUTER, out0)
    halo0.put(V, ext)
    send(1)

    narrow = pair_matrix(Z0, Z1, 0)
    narrow_low = pair_matrix(Z1, Z1, 0)
    narrow_high = pair_matrix(Z1, Z1, half)
    double01 = copy_matrix(Z1, Z0, 1)
    double12 = copy_matrix(Z1, Z1, 1)

    def restrict0(plane, factor, base, order=None):
        for x in order or range(X1):
            tall[base + x * R1 : base + (x + 1) * R1, :] = halve_rows(tmp, x, plane(2 * x) + plane(2 * x + 1))
        whole = dot(tall[base : base + X1 * R1, :], narrow) * factor
        return [whole[x * R1 : (x + 1) * R1] for x in range(X1)]

    def restrict1(plane, factor, order=None):
        rows = [None] * X2
        for x in order or range(X2):
            rows[x] = halve_rows(tmp, x, plane(2 * x) + plane(2 * x + 1))
        low = jnp.concatenate(rows[: X2 // 2], axis=0)
        high = jnp.concatenate(rows[X2 // 2 :], axis=0)
        return (dot(low, narrow_low) + dot(high, narrow_high)) * factor

    for x, val in enumerate(restrict0(lambda x: in0[x], 0.125, 0)):
        in1[x] = val
    for x, val in enumerate(restrict0(lambda x: out0[x], 0.125, 0)):
        out1[x] = val
    halo1.put(INNER1, in1)
    halo1.put(OUTER1, out1)
    send(2)
    gc_own[0] = restrict1(lambda x: in1[x], 0.125)
    gc_own[1] = restrict1(lambda x: out1[x], 0.125)
    gather_send(gc_own, gc, 0)

    for x in inner_first(0, X0):
        centre, near = halo0.neighbours(INNER, lambda x: in0[x], x, edge=True)
        u, near_u = halo0.neighbours(U, lambda x: uu[x], x)
        drive = jnp.zeros_like(u)
        for d in range(6):
            weight = jnp.minimum(centre, near[d])
            w0[d, x] = weight
            drive = drive + weight * (near_u[d] - u)
        m, r = mem[x], rec[x]
        tissue = jnp.where(label_of(x) != 0.0, 1.0, 0.0)
        ionic = ionic_gain * m * (m - ionic_onset) * (m - 1.0) + m * r
        mem_out[x] = m + TIME_STEP * (drive - tissue * ionic)
    publish(3, halo0, NEXT, mem_out)

    def scaled(grid, weights, centre, near, iz_edges):
        full = [weights[d] + 0.5 * (centre + near[d]) for d in range(6)]
        diag = ((full[0] + full[1]) + (full[2] + full[3])) + (full[4] + full[5])
        inv = 1.0 / diag
        full = [f * inv for f in full]
        low, high = iz_edges
        full[4] = jnp.where(low, 0.0, full[4])
        full[5] = jnp.where(high, 0.0, full[5])
        return full, diag, inv

    first0 = (g0.lane == 0) & (iz == 0)
    last0 = (g0.lane == Z0 - 1) & (iz == nz - 1)
    arrive(1)
    inv0 = vb
    for x in range(X0):
        centre, near = halo0.neighbours(OUTER, lambda x: out0[x], x, edge=True)
        full, diag, inv = scaled(g0, [w0[d, x] for d in range(6)], centre, near, (first0, last0))
        for d in range(6):
            c0[d, x] = full[d]
        d0[x] = diag
        b0[x] = inv

    def update(halo, slot, planes, c, b, x):
        val, near = halo.neighbours(slot, planes, x)
        a = b[x] + c[0, x] * near[0]
        e = c[1, x] * near[1] + c[2, x] * near[2]
        f = c[3, x] * near[3] + c[4, x] * near[4]
        return val, (a + c[5, x] * near[5]) + (e + f)

    def half_sweep(number, halo, slot, src, dst, c, b, colour):
        planes = halo.grid.planes
        for x in range(planes) if number is None else inner_first(number, planes):
            val, new = update(halo, slot, lambda x: src[x], c, b, x)
            dst[x] = jnp.where(halo.grid.colour(x, colour), new, val)

    for x in inner_first(3, X0):
        m, near = halo0.neighbours(NEXT, lambda x: mem_out[x], x)
        rhs = jnp.zeros_like(m)
        for d in range(6):
            rhs = rhs + w0[d, x] * (near[d] - m)
        b0[x] = rhs * b0[x]
        val, new = update(halo0, V, lambda x: ext[x], c0, b0, x)
        va[x] = jnp.where(g0.colour(x, 0), new, val)
    publish(4, halo0, RED, va)

    first1 = (g1.lane == 0) & (iz == 0)
    last1 = (g1.lane == Z1 - 1) & (iz == nz - 1)
    arrive(2)
    for x in range(X1):
        ci, ni = halo1.neighbours(INNER1, lambda x: in1[x], x, edge=True)
        co, no = halo1.neighbours(OUTER1, lambda x: out1[x], x, edge=True)
        full, diag, inv = scaled(g1, [jnp.minimum(ci, n) for n in ni], co, no, (first1, last1))
        for d in range(6):
            c1[d, x] = full[d]
        d1[x] = diag
        b1[x] = inv

    half_sweep(4, halo0, RED, va, vb, c0, b0, 1)
    publish(5, halo0, BLACK, vb)

    XG, RG, ZG = in2.shape
    XH, RH = XG // 2, RG // 2
    g2 = Grid(XG, RG, ZG)
    g3 = Grid(XH, RH, ZG)
    tile_row = lax.broadcasted_iota(jnp.int32, (8, LANES), 0)
    tile_lane = lax.broadcasted_iota(jnp.int32, (8, LANES), 1)

    def unpack(tile, dst):
        for px in range(nx):
            for py in range(ny // 2):
                lows, highs = [], []
                for part in range(2):
                    base = (px * ny + 2 * py + part) * nz
                    s0, s1 = tile(base), tile(base + 1)
                    lows.append(jnp.where(tile_lane < half, s0, pltpu.roll(s1, half, 1)))
                    highs.append(jnp.where(tile_lane < half, pltpu.roll(s0, half, 1), s1))
                for xhi, pair in enumerate((lows, highs)):
                    p = px * X2 + xhi * 2
                    dst[p, py * 8 : py * 8 + 8, :] = jnp.where(tile_row < R2, pair[0], pltpu.roll(pair[1], R2, 0))
                    dst[p + 1, py * 8 : py * 8 + 8, :] = jnp.where(
                        tile_row < R2, pltpu.roll(pair[0], R2, 0), pair[1]
                    )

    def whole_neighbours(grid, planes, x, last, mask):
        val = planes(x)
        zero = jnp.zeros_like(val)
        xm = planes(x - 1) if x > 0 else zero
        xp = planes(x + 1) if x < grid.planes - 1 else zero
        near = [
            xm,
            xp,
            pltpu.roll(val, 1, 0),
            pltpu.roll(val, grid.rows - 1, 0),
            pltpu.roll(val, 1, 1),
            pltpu.roll(val, grid.lanes - 1, 1),
        ]
        if mask:
            near[2] = jnp.where(grid.row == 0, 0.0, near[2])
            near[3] = jnp.where(grid.row == grid.rows - 1, 0.0, near[3])
            near[4] = jnp.where(grid.lane == 0, 0.0, near[4])
            near[5] = jnp.where(grid.lane >= last, 0.0, near[5])
        return val, near

    def whole_couplings(grid, inner, outer, last, c, d, b):
        for x in range(grid.planes):
            ci, ni = whole_neighbours(grid, lambda x: inner[x], x, last, True)
            co, no = whole_neighbours(grid, lambda x: outer[x], x, last, True)
            full = [jnp.minimum(ci, ni[k]) + 0.5 * (co + no[k]) for k in range(6)]
            diag = ((full[0] + full[1]) + (full[2] + full[3])) + (full[4] + full[5])
            if last < grid.lanes - 1:
                diag = jnp.where(grid.lane <= last, diag, 1.0)
            inv = 1.0 / diag
            edges = (
                None,
                None,
                grid.row == 0,
                grid.row == grid.rows - 1,
                grid.lane == 0,
                grid.lane >= last,
            )
            for k in range(6):
                f = full[k] * inv
                if edges[k] is not None:
                    f = jnp.where(edges[k], 0.0, f)
                if last < grid.lanes - 1:
                    f = jnp.where(grid.lane <= last, f, 0.0)
                c[k, x] = f
            if d is not None:
                d[x] = diag
            b[x] = inv

    def whole_update(grid, planes, c, b, x):
        val, near = whole_neighbours(grid, planes, x, None, False)
        a = b[x] + c[2, x] * near[2]
        e = c[3, x] * near[3] + c[4, x] * near[4]
        a = a + c[5, x] * near[5]
        if x > 0:
            a = a + c[0, x] * near[0]
        if x < grid.planes - 1:
            e = e + c[1, x] * near[1]
        return val, a + e

    def restrict2(plane, factor):
        pieces = [halve_rows(tmp, x, plane(2 * x) + plane(2 * x + 1)) for x in range(XH)]
        for x in range(XH):
            tall[x * RH : (x + 1) * RH, 0:ZG] = pieces[x]
        whole = dot(tall[0 : XH * RH, 0:ZG], narrow_low) * factor
        return [whole[x * RH : (x + 1) * RH] for x in range(XH)]

    gather_wait(gc, 0, True)
    unpack(lambda t: gc[t, 0], in2)
    unpack(lambda t: gc[t, 1], out2)
    whole_couplings(g2, in2, out2, ZG - 1, c2, d2, b2)
    for x, val in enumerate(restrict2(lambda x: in2[x], 0.125)):
        v3[x] = val
    for x, val in enumerate(restrict2(lambda x: out2[x], 0.125)):
        v2a[x, 0:RH] = val
    whole_couplings(g3, v3, v2a.at[:, 0:RH], ZG // 2 - 1, c3, None, b3)

    XP = XH // 2
    own = (g3.even, g3.odd)

    def pack(colour, near, far):
        return jnp.where(own[colour], near, far)

    for colour in range(2):
        for p in range(XP):
            a, z = 2 * p, 2 * p + 1
            k3[colour * 6, p] = pack(colour, c3[1, a], c3[0, z])
            k3[colour * 6 + 1, p] = pack(colour, c3[0, a], c3[1, z])
            for k in range(2, 6):
                k3[colour * 6 + k, p] = pack(colour, c3[k, a], c3[k, z])

    def residual0(x):
        val, new = update(halo0, BLACK, lambda x: vb[x], c0, b0, x)
        return d0[x] * (new - val)

    for x, val in enumerate(restrict0(residual0, 0.5, 0, inner_first(5, X1))):
        b1[x] = val * b1[x]
        v1a[x] = jnp.where(g1.colour(x, 0), b1[x], 0.0)
    publish(6, halo1, RED1, v1a)
    half_sweep(6, halo1, RED1, v1a, v1b, c1, b1, 1)
    publish(7, halo1, BLACK1, v1b)

    def residual1(x):
        val, new = update(halo1, BLACK1, lambda x: v1b[x], c1, b1, x)
        return d1[x] * (new - val)

    gr_own[...] = restrict1(residual1, 0.5, inner_first(7, X2))
    gather_send(gr_own, gr, 1)
    gather_wait(gr, 1, True)
    unpack(lambda t: gr[t], v2b)
    for x in range(XG):
        b2[x] = v2b[x] * b2[x]
        v2a[x] = jnp.where(g2.colour(x, 0), b2[x], 0.0)
    for x in range(XG):
        val, new = whole_update(g2, lambda x: v2a[x], c2, b2, x)
        v2b[x] = jnp.where(g2.colour(x, 1), new, val)

    def residual2(x):
        val, new = whole_update(g2, lambda x: v2b[x], c2, b2, x)
        return d2[x] * (new - val)

    for x, val in enumerate(restrict2(residual2, 0.5)):
        b3[x] = val * b3[x]

    for colour in range(2):
        for p in range(XP):
            h3[colour, p] = pack(colour, b3[2 * p], b3[2 * p + 1])
    none = jnp.zeros((RH, ZG), F32)

    def relaxed(colour, other):
        fresh = []
        for p in range(XP):
            val, at = other[p], colour * 6
            before = other[p - 1] if p > 0 else none
            after = other[p + 1] if p < XP - 1 else none
            i = h3[colour, p] + k3[at, p] * val
            j = k3[at + 1, p] * pack(colour, before, after) + k3[at + 2, p] * pltpu.roll(val, 1, 0)
            l = k3[at + 3, p] * pltpu.roll(val, RH - 1, 0) + k3[at + 4, p] * pltpu.roll(val, 1, 1)
            fresh.append((i + k3[at + 5, p] * pltpu.roll(val, ZG - 1, 1)) + (j + l))
        return fresh

    def coarse(step, state):
        red = relaxed(0, state[XP:])
        black = relaxed(1, red)
        return tuple(red + black)

    state = lax.fori_loop(0, COARSE_SWEEPS, coarse, (none,) * (2 * XP))
    solved = []
    for p in range(XP):
        solved.append(pack(0, state[p], state[XP + p]))
        solved.append(pack(1, state[p], state[XP + p]))
    for x in range(XH):
        tall[x * RH : (x + 1) * RH, 0:ZG] = solved[x]
    wide = dot(tall[0 : XH * RH, 0:ZG], double12)
    for x in range(XH):
        corr = double_rows(tmp, x, wide[x * RH : (x + 1) * RH])
        v2a[2 * x] = v2b[2 * x] + corr
        v2a[2 * x + 1] = v2b[2 * x + 1] + corr
    for colour, src, dst in ((0, v2a, v2b), (1, v2b, v2a)):
        for x in range(XG):
            val, new = whole_update(g2, lambda x: src[x], c2, b2, x)
            dst[x] = jnp.where(g2.colour(x, colour), new, val)

    row_shift = lax.rem(RG - iy * R2, RG)
    lane_shift = lax.rem(ZG - iz * half, ZG)
    lane8 = lax.broadcasted_iota(jnp.int32, (8, LANES), 1)
    side = jnp.zeros((8, LANES), F32)
    below, above = X2 * 8, X2 * 8 + 8
    low, high, across = above + 8, above + 16, above + 24
    tall[low : across, 0:ZG] = jnp.zeros((across - low, ZG), F32)
    for k in range(-1, X2 + 1):
        part = v2a[jnp.clip(ix * X2 + k, 0, XG - 1)]
        part = pltpu.roll(pltpu.roll(part, row_shift, 0), lane_shift, 1)
        if k < 0:
            tall[below : below + 8, 0:ZG] = jnp.where(ix > 0, part[0:8], 0.0)
        elif k == X2:
            tall[above : above + 8, 0:ZG] = jnp.where(ix < nx - 1, part[0:8], 0.0)
        else:
            tall[k * 8 : (k + 1) * 8, 0:ZG] = part[0:8]
            tall[low + k : low + k + 1, 0:ZG] = jnp.where(iy > 0, part[RG - 1 : RG], 0.0)
            tall[high + k : high + k + 1, 0:ZG] = jnp.where(iy < ny - 1, part[R2 : R2 + 1], 0.0)
            turned = pltpu.roll(part[0:8], k + 1 + (half - 1) * (1 - iz), 1)
            side = jnp.where(lane8 == k, turned, side)
    tall[across : across + 8, 0:ZG] = side
    wide = dot(tall[0 : across + 8, 0:ZG], double12)

    def grown(slot, row):
        return double_rows(tmp, slot, wide[row : row + R2])

    for x in range(X2):
        corr = grown(x, x * 8)
        v1a[2 * x] = v1b[2 * x] + corr
        v1a[2 * x + 1] = v1b[2 * x + 1] + corr
    xh1[0, FIXED1] = xh1[0, BLACK1] + grown(0, below)
    xh1[1, FIXED1] = xh1[1, BLACK1] + grown(1, above)
    yh1[0, FIXED1] = yh1[0, BLACK1] + grown(2, low)
    yh1[1, FIXED1] = yh1[1, BLACK1] + grown(3, high)
    zh1[FIXED1] = zh1[BLACK1] + grown(0, across)
    half_sweep(None, halo1, FIXED1, v1a, v1b, c1, b1, 0)
    publish(8, halo1, LASTRED1, v1b)
    half_sweep(8, halo1, LASTRED1, v1b, v1a, c1, b1, 1)
    publish(9, halo1, LASTBLACK1, v1a)

    def enlarge(count, read, write):
        for x in range(count):
            tall[x * R1 : (x + 1) * R1, 0:Z1] = read(x)
        wide = dot(tall[0 : count * R1, 0:Z1], double01)
        for x in range(count):
            write(x, double_rows(tmp, x, wide[x * R1 : (x + 1) * R1]))

    def inside(x, corr):
        va[2 * x] = vb[2 * x] + corr
        va[2 * x + 1] = vb[2 * x + 1] + corr

    enlarge(X1, lambda x: v1a[x], inside)
    arrive(9)

    def rim(k):
        if k < 2:
            return xh1[k, LASTBLACK1]
        if k < 4:
            return yh1[k - 2, LASTBLACK1]
        return zh1[LASTBLACK1]

    def outside(k, corr):
        if k < 2:
            xh0[k, FIXED] = xh0[k, BLACK] + corr
        elif k < 4:
            yh0[k - 2, FIXED] = yh0[k - 2, BLACK] + corr
        else:
            zh0[FIXED] = zh0[BLACK] + corr[:, 0:LANES]

    enlarge(5, rim, outside)
    half_sweep(None, halo0, FIXED, va, vb, c0, b0, 0)
    publish(10, halo0, LAST, vb)
    half_sweep(10, halo0, LAST, vb, ext_out, c0, b0, 1)

    for number in range(len(EXCHANGES)):
        sent(number)
    gather_wait(gc, 0, False)
    gather_wait(gr, 1, False)


def finish(mem, rec, mem_in, ext_in, mem_out, rec_out, ext_out):
    mem_out[...] = mem_in[...]
    ext_out[...] = ext_in[...]
    m, r = mem[...], rec[...]
    rec_out[...] = r + TIME_STEP * recovery_rate * (-r - ionic_gain * m * (m - ionic_onset - 1.0))


def solution(mesh):
    nx, ny, nz = (mesh.shape[a] for a in ("gx", "gy", "gz"))
    spec = P("gx", "gy", "gz")

    def on_device(membrane, recovery, extracellular, fiber_scale, labels):
        X, R, Z = membrane.shape
        X1, R1, Z1 = X // 2, R // 2, Z // 2
        XG, RG, ZG = nx * X // 4, ny * R // 4, nz * Z // 4
        assert nz == 2 and ny % 2 == 0 and ZG == LANES and Z1 == LANES
        assert R1 == 8 and X1 == 8 and X % 8 == 0
        total = nx * ny * nz
        f0, f1 = 9, 7
        field = (X, R, Z)
        lvl1 = (X1, R1, Z1)
        whole = (XG, RG, ZG)
        third = (XG // 2, RG // 2, ZG)

        def v(*shape):
            return pltpu.VMEM(shape, F32)

        def faces(f, x, r, z):
            return [v(2, f, r, z), v(2, f, x, z), v(f, r, LANES)] * 2

        scratch = faces(f0, *field) + faces(f1, *lvl1)
        scratch += [v(*field), v(*field), v(*field), v(6, *field), v(6, *field), v(*field), v(*field)]
        scratch += [v(*field), v(*field)]
        scratch += [
            v(2 * max(X1, XG // 2), max(R, RG), LANES),
            v(max(X1 * R1, (XG // 2) * (RG // 2), 2 * X1 * R1), Z),
        ]
        scratch += [v(*lvl1), v(*lvl1), v(6, *lvl1), v(*lvl1), v(*lvl1), v(*lvl1), v(*lvl1)]
        scratch += [v(2, 8, LANES), v(total, 2, 8, LANES), v(8, LANES), v(total, 8, LANES)]
        scratch += [v(*whole), v(*whole), v(6, *whole), v(*whole), v(*whole), v(*whole), v(*whole)]
        scratch += [v(6, *third), v(*third), v(*third)]
        packed = (XG // 4, RG // 2, ZG)
        scratch += [v(12, *packed), v(2, *packed)]
        sems = SIDES * len(EXCHANGES)
        scratch += [pltpu.SemaphoreType.DMA((sems,))] * 2 + [pltpu.SemaphoreType.DMA((2,))] * 2
        vmem = pl.BlockSpec(memory_space=pltpu.VMEM)
        field_bytes = 4 * XG * RG * ZG
        shape = jax.ShapeDtypeStruct(field, F32)
        mem_next, ext_next = pl.pallas_call(
            functools.partial(kernel, (nx, ny, nz)),
            out_shape=[shape] * 2,
            in_specs=[vmem] * 5,
            out_specs=[vmem] * 2,
            scratch_shapes=scratch,
            compiler_params=pltpu.CompilerParams(
                collective_id=0, has_side_effects=True, vmem_limit_bytes=(16 << 20) + 16 * field_bytes
            ),
        )(membrane, recovery, extracellular, fiber_scale, labels)
        return tuple(
            pl.pallas_call(
                finish,
                out_shape=[shape] * 3,
                in_specs=[vmem] * 4,
                out_specs=[vmem] * 3,
                compiler_params=pltpu.CompilerParams(vmem_limit_bytes=4 << 20),
            )(membrane, recovery, mem_next, ext_next)
        )

    return jax.shard_map(
        on_device,
        mesh=mesh,
        in_specs=(spec,) * 5,
        out_specs=(spec,) * 3,
        check_vma=False,
    )
```

profile of v0, /device:TPU:0, one launch (start us, length us, event | category | flops | bytes accessed | tf_op | source)
XLA Modules:
  0.0 54.4 jit_solution(8800346173725675574)
XLA Ops:
  0.6 0.0 copy-start
  0.6 0.9 %copy-done = f32[16,16,256]{2,1,0:T(8,128)S(1)} copy-done((f32[16,16,256]{2,1,0:T(8,128)S(1)}, f32[16,16,256]{2,1,0:T(8,128)}, u32[]{:S(2)}) %copy-start) | copy-done | bytes 262168
  1.6 0.0 copy-start.1
  1.6 0.9 %copy-done.1 = f32[16,16,256]{2,1,0:T(8,128)S(1)} copy-done((f32[16,16,256]{2,1,0:T(8,128)S(1)}, f32[16,16,256]{2,1,0:T(8,128)}, u32[]{:S(2)}) %copy-start.1) | copy-done | bytes 262168
  2.5 0.0 copy-start.2
  2.5 0.9 %copy-done.2 = f32[16,16,256]{2,1,0:T(8,128)S(1)} copy-done((f32[16,16,256]{2,1,0:T(8,128)S(1)}, f32[16,16,256]{2,1,0:T(8,128)}, u32[]{:S(2)}) %copy-start.2) | copy-done | bytes 262168
  3.5 0.0 copy-start.3
  3.5 0.9 %copy-done.3 = f32[16,16,256]{2,1,0:T(8,128)S(1)} copy-done((f32[16,16,256]{2,1,0:T(8,128)S(1)}, f32[16,16,256]{2,1,0:T(8,128)}, u32[]{:S(2)}) %copy-start.3) | copy-done | bytes 262168
  4.4 0.0 copy-start.4
  4.4 0.7 %copy-done.4 = s32[2,2,32]{2,1,0:T(2,128)S(1)} copy-done((s32[2,2,32]{2,1,0:T(2,128)S(1)}, s32[2,2,32]{2,1,0:T(2,128)}, u32[]{:S(2)}) %copy-start.4) | copy-done | bytes 536
  5.1 48.3 %shard_map.76 = (f32[16,16,256]{2,1,0:T(8,128)S(1)}, f32[16,16,256]{2,1,0:T(8,128)S(1)}) custom-call(f32[16,16,256]{2,1,0:T(8,128)S(1)} %copy-done, f32[16,16,256]{2,1,0:T(8,128)S(1)} %copy-done.1, f32[16,16,256]{2,1,0:T(8,128)S(1)} %copy-done.2, f32[16,16,256]{2,1,0:T(8,128)S(1)} %copy-done.3, s32[2,2,32]{2,1,0:T(2,128)S(1)} %copy-done.4), custom_call_target="tpu_custom_call" | custom-call | tf_op jit(solution)/shard_map/pallas_call | solution.py:708
  53.5 1.0 %shard_map.77 = (f32[16,16,256]{2,1,0:T(8,128)}, f32[16,16,256]{2,1,0:T(8,128)}, f32[16,16,256]{2,1,0:T(8,128)}) custom-call(f32[16,16,256]{2,1,0:T(8,128)S(1)} %copy-done, f32[16,16,256]{2,1,0:T(8,128)S(1)} %copy-done.1, f32[16,16,256]{2,1,0:T(8,128)S(1)} %get-tuple-element.5.mem_in, f32[16,16,256]{2,1,0:T(8,128)S(1)} %get-tuple-element.6.ext_in), custom_call_target="tpu_custom_call" | custom-call | tf_op jit(solution)/shard_map/pallas_call | solution.py:719
Async XLA Ops:
  0.6 1.0 %copy-start = (f32[16,16,256]{2,1,0:T(8,128)S(1)}, f32[16,16,256]{2,1,0:T(8,128)}, u32[]{:S(2)}) copy-start(f32[16,16,256]{2,1,0:T(8,128)} %mem.1) | copy-start | bytes 786436
  1.6 0.9 %copy-start.1 = (f32[16,16,256]{2,1,0:T(8,128)S(1)}, f32[16,16,256]{2,1,0:T(8,128)}, u32[]{:S(2)}) copy-start(f32[16,16,256]{2,1,0:T(8,128)} %rec.1) | copy-start | bytes 786436
  2.5 0.9 %copy-start.2 = (f32[16,16,256]{2,1,0:T(8,128)S(1)}, f32[16,16,256]{2,1,0:T(8,128)}, u32[]{:S(2)}) copy-start(f32[16,16,256]{2,1,0:T(8,128)} %refs_2_.1) | copy-start | bytes 786436
  3.5 0.9 %copy-start.3 = (f32[16,16,256]{2,1,0:T(8,128)S(1)}, f32[16,16,256]{2,1,0:T(8,128)}, u32[]{:S(2)}) copy-start(f32[16,16,256]{2,1,0:T(8,128)} %refs_3_.1) | copy-start | bytes 786436
  4.4 0.7 %copy-start.4 = (s32[2,2,32]{2,1,0:T(2,128)S(1)}, s32[2,2,32]{2,1,0:T(2,128)}, u32[]{:S(2)}) copy-start(s32[2,2,32]{2,1,0:T(2,128)} %refs_4_.1) | copy-start | bytes 1540
where the time goes:
time: 54.7 us; the launch traced here: 54.4 us
  Pallas kernels  49.3 us (90%)
  local copies, waits for them, and re-layouts  4.47 us (8%)
  between operations  0.65 us (1%)
    pallas_call x1, Pallas kernels, on_device(): pl.pallas_call(functools.partial(kernel, (nx, ny, nz)), out_shape=[shape]...  48.3 us
    unnamed x10, local copies, waits for them, and re-layouts  4.47 us

commit v1 on v0

--- a/solution.py
+++ b/solution.py
@@ -137,7 +137,10 @@
 
 
 def kernel(counts, *refs):
-    (mem, rec, ext, fib, lab, mem_out, ext_out) = refs[:7]
+    sources, (mem_out, rec_out, ext_out) = refs[:5], refs[5:8]
+    refs = refs[8:]
+    mem, rec, ext, fib, lab, in_sem = refs[:6]
+    refs = (None,) + refs
     (xs0, ys0, zs0, xh0, yh0, zh0, xs1, ys1, zs1, xh1, yh1, zh1) = refs[7:19]
     (in0, out0, uu, w0, c0, d0, b0, va, vb, tmp, tall) = refs[19:30]
     (in1, out1, c1, d1, b1, v1a, v1b) = refs[30:37]
@@ -148,8 +151,12 @@
     me = (ix * ny + iy) * nz + iz
     total = nx * ny * nz
 
-    for ref in (xh0, yh0, xh1, yh1):
-        ref[...] = jnp.zeros(ref.shape, F32)
+    loads = [
+        pltpu.make_async_copy(src, dst, in_sem.at[i])
+        for i, (src, dst) in enumerate(zip(sources, (mem, rec, ext, fib, lab)))
+    ]
+    for i in (4, 3, 0, 2, 1):
+        loads[i].start()
 
     barrier = pltpu.get_barrier_semaphore()
 
@@ -162,6 +169,20 @@
         lax.fori_loop(1, total, step, 0)
 
     others(lambda dev, where: pl.semaphore_signal(barrier, inc=1, device_id=where, device_id_type=MESH))
+
+    def clear(missing, ref, side):
+        def fill():
+            ref[side] = jnp.zeros(ref.shape[1:], F32)
+
+        pl.when(missing)(fill)
+
+    for xh, yh in ((xh0, yh0), (xh1, yh1)):
+        clear(ix == 0, xh, 0)
+        clear(ix == nx - 1, xh, 1)
+        clear(iy == 0, yh, 0)
+        clear(iy == ny - 1, yh, 1)
+    for load in loads:
+        load.wait()
 
     g0 = Grid(*mem.shape)
     g1 = Grid(*in1.shape)
@@ -331,6 +352,9 @@
         ionic = ionic_gain * m * (m - ionic_onset) * (m - 1.0) + m * r
         mem_out[x] = m + TIME_STEP * (drive - tissue * ionic)
     publish(3, halo0, NEXT, mem_out)
+    for x in range(X0):
+        m, r = mem[x], rec[x]
+        rec_out[x] = r + TIME_STEP * recovery_rate * (-r - ionic_gain * m * (m - ionic_onset - 1.0))
 
     def scaled(grid, weights, centre, near, iz_edges):
         full = [weights[d] + 0.5 * (centre + near[d]) for d in range(6)]
@@ -657,11 +681,14 @@
     gather_wait(gr, 1, False)
 
 
-def finish(mem, rec, mem_in, ext_in, mem_out, rec_out, ext_out):
-    mem_out[...] = mem_in[...]
-    ext_out[...] = ext_in[...]
-    m, r = mem[...], rec[...]
-    rec_out[...] = r + TIME_STEP * recovery_rate * (-r - ionic_gain * m * (m - ionic_onset - 1.0))
+def finish(*refs):
+    count = (len(refs) - 1) // 2
+    sem = refs[-1]
+    copies = [pltpu.make_async_copy(refs[i], refs[count + i], sem.at[i]) for i in range(count)]
+    for copy in copies:
+        copy.start()
+    for copy in copies:
+        copy.wait()
 
 
 def solution(mesh):
@@ -687,7 +714,9 @@
         def faces(f, x, r, z):
             return [v(2, f, r, z), v(2, f, x, z), v(f, r, LANES)] * 2
 
-        scratch = faces(f0, *field) + faces(f1, *lvl1)
+        anywhere = pl.BlockSpec(memory_space=pl.ANY)
+        scratch = [v(*field)] * 4 + [pltpu.VMEM(labels.shape, jnp.int32), pltpu.SemaphoreType.DMA((5,))]
+        scratch += faces(f0, *field) + faces(f1, *lvl1)
         scratch += [v(*field), v(*field), v(*field), v(6, *field), v(6, *field), v(*field), v(*field)]
         scratch += [v(*field), v(*field)]
         scratch += [
@@ -703,26 +732,27 @@
         sems = SIDES * len(EXCHANGES)
         scratch += [pltpu.SemaphoreType.DMA((sems,))] * 2 + [pltpu.SemaphoreType.DMA((2,))] * 2
         vmem = pl.BlockSpec(memory_space=pltpu.VMEM)
-        field_bytes = 4 * XG * RG * ZG
+        room = 54400 << 10
         shape = jax.ShapeDtypeStruct(field, F32)
-        mem_next, ext_next = pl.pallas_call(
+        results = pl.pallas_call(
             functools.partial(kernel, (nx, ny, nz)),
-            out_shape=[shape] * 2,
-            in_specs=[vmem] * 5,
-            out_specs=[vmem] * 2,
+            out_shape=[shape] * 3,
+            in_specs=[anywhere] * 5,
+            out_specs=[vmem] * 3,
             scratch_shapes=scratch,
             compiler_params=pltpu.CompilerParams(
-                collective_id=0, has_side_effects=True, vmem_limit_bytes=(16 << 20) + 16 * field_bytes
+                collective_id=0, has_side_effects=True, vmem_limit_bytes=room
             ),
         )(membrane, recovery, extracellular, fiber_scale, labels)
         return tuple(
             pl.pallas_call(
                 finish,
                 out_shape=[shape] * 3,
-                in_specs=[vmem] * 4,
-                out_specs=[vmem] * 3,
+                in_specs=[vmem] * 3,
+                out_specs=[anywhere] * 3,
+                scratch_shapes=[pltpu.SemaphoreType.DMA((3,))],
                 compiler_params=pltpu.CompilerParams(vmem_limit_bytes=4 << 20),
-            )(membrane, recovery, mem_next, ext_next)
+            )(*results)
         )
 
     return jax.shard_map(

time: 54.7 us -> 50.6 us (0.925)
  local copies, waits for them, and re-layouts: 4.47 us -> 0.67 us
    unnamed x10 -> x2, local copies, waits for them, and re-layouts: 4.47 us -> 0.67 us
where the time goes in v1:
time: 50.6 us; the launch traced here: 50.4 us
  Pallas kernels  49.1 us (97%)
  local copies, waits for them, and re-layouts  0.67 us (1%)
  between operations  0.65 us (1%)
    pallas_call x1, Pallas kernels, on_device(): pl.pallas_call(functools.partial(kernel, (nx, ny, nz)), out_shape=[shape]...  48.2 us

profile of v1, /device:TPU:0, one launch (start us, length us, event | category | flops | bytes accessed | tf_op | source)
XLA Modules:
  0.0 50.4 jit_solution(8801654538929513290)
XLA Ops:
  0.6 0.0 copy-start
  0.6 0.7 %copy-done = s32[2,2,32]{2,1,0:T(2,128)S(1)} copy-done((s32[2,2,32]{2,1,0:T(2,128)S(1)}, s32[2,2,32]{2,1,0:T(2,128)}, u32[]{:S(2)}) %copy-start) | copy-done | bytes 536
  1.3 48.2 %shard_map.76 = (f32[16,16,256]{2,1,0:T(8,128)S(1)}, f32[16,16,256]{2,1,0:T(8,128)S(1)}, f32[16,16,256]{2,1,0:T(8,128)S(1)}) custom-call(f32[16,16,256]{2,1,0:T(8,128)} %refs_0_.1, f32[16,16,256]{2,1,0:T(8,128)} %refs_1_.1, f32[16,16,256]{2,1,0:T(8,128)} %refs_2_.1, f32[16,16,256]{2,1,0:T(8,128)} %refs_3_.1, s32[2,2,32]{2,1,0:T(2,128)S(1)} %copy-done), custom_call_target="tpu_custom_call" | custom-call | tf_op jit(solution)/shard_map/pallas_call | solution.py:737
  49.5 0.9 %shard_map.77 = (f32[16,16,256]{2,1,0:T(8,128)}, f32[16,16,256]{2,1,0:T(8,128)}, f32[16,16,256]{2,1,0:T(8,128)}) custom-call(f32[16,16,256]{2,1,0:T(8,128)S(1)} %get-tuple-element.6.refs_0_, f32[16,16,256]{2,1,0:T(8,128)S(1)} %get-tuple-element.7.refs_1_, f32[16,16,256]{2,1,0:T(8,128)S(1)} %get-tuple-element.8.refs_2_), custom_call_target="tpu_custom_call" | custom-call | tf_op jit(solution)/shard_map/pallas_call | solution.py:748
Async XLA Ops:
  0.6 0.7 %copy-start = (s32[2,2,32]{2,1,0:T(2,128)S(1)}, s32[2,2,32]{2,1,0:T(2,128)}, u32[]{:S(2)}) copy-start(s32[2,2,32]{2,1,0:T(2,128)} %refs_4_.1) | copy-start | bytes 1540

commit v2 on v1

--- a/solution.py
+++ b/solution.py
@@ -17,21 +17,20 @@
 F32 = jnp.float32
 
 INNER, U, OUTER, V, NEXT, RED, BLACK, FIXED, LAST = range(9)
-INNER1, OUTER1, RED1, BLACK1, FIXED1, LASTRED1, LASTBLACK1 = range(7)
+INNER1, OUTER1, RHS1 = range(3)
+GHOST = 4
 EXCHANGES = (
-    (0, INNER, 2),
-    (0, OUTER, 2),
-    (1, INNER1, 2),
-    (0, NEXT, 1),
-    (0, RED, 1),
-    (0, BLACK, 1),
-    (1, RED1, 1),
-    (1, BLACK1, 1),
-    (1, LASTRED1, 1),
-    (1, LASTBLACK1, 1),
-    (0, LAST, 1),
+    (INNER, 2),
+    (OUTER, 2),
+    (NEXT, 1),
+    (RED, 1),
+    (BLACK, 1),
+    (LAST, 1),
 )
 SIDES = 5
+WIDE = ((INNER1, 2), (RHS1, 1))
+STEPS = (-1, 0, 1)
+WIDE_SIDES = 17
 
 
 def dot(a, b):
@@ -141,11 +140,11 @@
     refs = refs[8:]
     mem, rec, ext, fib, lab, in_sem = refs[:6]
     refs = (None,) + refs
-    (xs0, ys0, zs0, xh0, yh0, zh0, xs1, ys1, zs1, xh1, yh1, zh1) = refs[7:19]
-    (in0, out0, uu, w0, c0, d0, b0, va, vb, tmp, tall) = refs[19:30]
-    (in1, out1, c1, d1, b1, v1a, v1b) = refs[30:37]
-    (gc_own, gc, gr_own, gr, in2, out2, c2, d2, b2, v2a, v2b) = refs[37:48]
-    (c3, b3, v3, k3, h3, send_sem, recv_sem, gs_sem, gr_sem) = refs[48:]
+    (xs0, ys0, zs0, xh0, yh0, zh0) = refs[7:13]
+    (in0, out0, uu, w0, c0, d0, b0, va, vb, tmp, tall) = refs[13:24]
+    (ee, ys1, yr1, zs1, zr1, zp1, c1, cz1, d1, b1, v1a, v1b, z1a, z1b, yrim) = refs[24:39]
+    (gc_own, gc, gr_own, gr, in2, out2, c2, d2, b2, v2a, v2b) = refs[39:50]
+    (c3, b3, v3, k3, h3, send_sem, recv_sem, wide_send, wide_recv, gs_sem, gr_sem) = refs[50:]
     nx, ny, nz = counts
     ix, iy, iz = lax.axis_index("gx"), lax.axis_index("gy"), lax.axis_index("gz")
     me = (ix * ny + iy) * nz + iz
@@ -172,26 +171,30 @@
 
     def clear(missing, ref, side):
         def fill():
-            ref[side] = jnp.zeros(ref.shape[1:], F32)
+            ref[side] = jnp.zeros(ref.at[side].shape, F32)
 
         pl.when(missing)(fill)
 
-    for xh, yh in ((xh0, yh0), (xh1, yh1)):
-        clear(ix == 0, xh, 0)
-        clear(ix == nx - 1, xh, 1)
-        clear(iy == 0, yh, 0)
-        clear(iy == ny - 1, yh, 1)
+    X1, R1, Z1 = mem.shape[0] // 2, mem.shape[1] // 2, mem.shape[2] // 2
+    XE, RE = X1 + 2 * GHOST, R1 + 2 * GHOST
+    clear(ix == 0, xh0, 0)
+    clear(ix == nx - 1, xh0, 1)
+    clear(iy == 0, yh0, 0)
+    clear(iy == ny - 1, yh0, 1)
+    for slot in range(3):
+        for p in range(GHOST):
+            clear(ix == 0, ee, (slot, p))
+            clear(ix == nx - 1, ee, (slot, XE - 1 - p))
     for load in loads:
         load.wait()
 
     g0 = Grid(*mem.shape)
-    g1 = Grid(*in1.shape)
+    g1 = Grid(XE, RE, Z1)
     halo0 = Halo(g0, (xs0, ys0, zs0, xh0, yh0, zh0), iz)
-    halo1 = Halo(g1, (xs1, ys1, zs1, xh1, yh1, zh1), iz)
 
     def copies(number):
-        level, first, slots = EXCHANGES[number]
-        h = (halo0, halo1)[level]
+        first, slots = EXCHANGES[number]
+        h = halo0
         part = pl.ds(first, slots)
         plan = (
             (h.xs.at[0, part], h.xh.at[1, part], (ix - 1, iy, iz), ix > 0, ix < nx - 1),
@@ -247,6 +250,106 @@
             else:
                 pl.when(goes)(copy.wait_send)
 
+    here = {-1: ix > 0, 0: None, 1: ix < nx - 1}
+    along = {-1: iy > 0, 0: None, 1: iy < ny - 1}
+
+    def both(a, b):
+        if a is None or b is None:
+            return b if a is None else a
+        return jnp.logical_and(a, b)
+
+    def wide_copies(number):
+        first, count = WIDE[number]
+        part = pl.ds(first, count)
+        pairs, edge = X1 // 2, GHOST // 2
+        plan = []
+        for sx in (-1, 1):
+            src = ee.at[part, pl.ds(GHOST if sx < 0 else X1, GHOST), pl.ds(0, R1)]
+            dst = ee.at[part, pl.ds(X1 + GHOST if sx < 0 else 0, GHOST), pl.ds(0, R1)]
+            plan.append((src, dst, sx, 0, iz))
+        for sx in STEPS:
+            for sy in (-1, 1):
+                mine, theirs = (0, 1) if sy < 0 else (1, 0)
+                at = {-1: (0, edge, pairs + edge), 0: (0, pairs, edge), 1: (pairs - edge, edge, 0)}[sx]
+                src = ys1.at[mine, part, pl.ds(at[0], at[1])]
+                dst = yr1.at[theirs, part, pl.ds(at[2], at[1])]
+                plan.append((src, dst, sx, sy, iz))
+        for sx in STEPS:
+            for sy in STEPS:
+                plan.append((zs1.at[part], zr1.at[(1 - sx) * 3 + 1 - sy, part], sx, sy, 1 - iz))
+        for side, (src, dst, sx, sy, z) in enumerate(plan):
+            copy = pltpu.make_async_remote_copy(
+                src_ref=src,
+                dst_ref=dst,
+                send_sem=wide_send.at[number * WIDE_SIDES + side],
+                recv_sem=wide_recv.at[number * WIDE_SIDES + side],
+                device_id=(ix + sx, iy + sy, z),
+                device_id_type=MESH,
+            )
+            yield copy, both(here[sx], along[sy]), both(here[-sx], along[-sy])
+
+    def maybe(condition, action):
+        if condition is None:
+            action()
+        else:
+            pl.when(condition)(action)
+
+    tile_row = lax.broadcasted_iota(jnp.int32, (8, LANES), 0)
+    tile_lane = lax.broadcasted_iota(jnp.int32, (8, LANES), 1)
+
+    def wide_publish(number):
+        first, count = WIDE[number]
+        for slot in range(first, first + count):
+            acc = jnp.zeros((R1, LANES), F32)
+            for x in range(X1):
+                val = ee[slot, GHOST + x, 0:R1, :]
+                for depth in range(GHOST):
+                    at = depth * XE + GHOST + x
+                    shift = jnp.where(iz == 0, at + 1 + depth, at - depth)
+                    acc = jnp.where(tile_lane == at, pltpu.roll(val, shift, 1), acc)
+            zs1[slot] = acc
+            for k in range(X1 // 2):
+                even, odd = ee[slot, GHOST + 2 * k, 0:R1, :], ee[slot, GHOST + 2 * k + 1, 0:R1, :]
+                ys1[0, slot, k] = jnp.where(tile_row < GHOST, even, pltpu.roll(odd, GHOST, 0))
+                ys1[1, slot, k] = jnp.where(tile_row < GHOST, pltpu.roll(odd, GHOST, 0), even)
+        for copy, goes, _ in wide_copies(number):
+            maybe(goes, copy.start)
+
+    def keep(condition, val):
+        return val if condition is None else jnp.where(condition, val, 0.0)
+
+    def plane_side(p):
+        return here[-1 if p < GHOST else (1 if p >= X1 + GHOST else 0)]
+
+    def wide_arrive(number):
+        first, count = WIDE[number]
+        for copy, _, comes in wide_copies(number):
+            maybe(comes, copy.wait_recv)
+        low = tile_row >= GHOST
+        pe = jnp.bitwise_and(tile_lane, XE - 1)
+        for slot in range(first, first + count):
+            for p in range(XE):
+                after, before = yr1[1, slot, p // 2], yr1[0, slot, p // 2]
+                if p % 2:
+                    after, before = pltpu.roll(after, GHOST, 0), pltpu.roll(before, GHOST, 0)
+                side = plane_side(p)
+                after = keep(both(side, along[1]), after)
+                before = keep(both(side, along[-1]), before)
+                ee[slot, p, R1:RE, :] = jnp.where(low, before, after)
+            rows = []
+            for sy in STEPS:
+                mid = zr1[3 + sy + 1, slot]
+                left = keep(here[-1], pltpu.roll(zr1[sy + 1, slot], LANES - X1, 1))
+                right = keep(here[1], pltpu.roll(zr1[6 + sy + 1, slot], X1, 1))
+                val = jnp.where(pe < GHOST, left, jnp.where(pe >= X1 + GHOST, right, mid))
+                rows.append(keep(along[sy], jnp.where(tile_lane < GHOST * XE, val, 0.0)))
+            zp1[slot, 0:R1, :] = rows[1]
+            zp1[slot, R1:RE, :] = jnp.where(low, rows[0], rows[2])
+
+    def wide_sent(number):
+        for copy, goes, _ in wide_copies(number):
+            maybe(goes, copy.wait_send)
+
     def gather_send(own, whole, which):
         def go(dev, where):
             pltpu.make_async_remote_copy(
@@ -277,7 +380,6 @@
             copy.wait_send()
 
     X0, R0, Z0 = mem.shape
-    X1, R1, Z1 = in1.shape
     X2 = X1 // 2
     R2 = R1 // 2
     half = Z1 // 2
@@ -329,14 +431,12 @@
         return (dot(low, narrow_low) + dot(high, narrow_high)) * factor
 
     for x, val in enumerate(restrict0(lambda x: in0[x], 0.125, 0)):
-        in1[x] = val
+        ee[INNER1, GHOST + x, 0:R1, :] = val
     for x, val in enumerate(restrict0(lambda x: out0[x], 0.125, 0)):
-        out1[x] = val
-    halo1.put(INNER1, in1)
-    halo1.put(OUTER1, out1)
-    send(2)
-    gc_own[0] = restrict1(lambda x: in1[x], 0.125)
-    gc_own[1] = restrict1(lambda x: out1[x], 0.125)
+        ee[OUTER1, GHOST + x, 0:R1, :] = val
+    wide_publish(0)
+    gc_own[0] = restrict1(lambda x: ee[INNER1, GHOST + x, 0:R1, :], 0.125)
+    gc_own[1] = restrict1(lambda x: ee[OUTER1, GHOST + x, 0:R1, :], 0.125)
     gather_send(gc_own, gc, 0)
 
     for x in inner_first(0, X0):
@@ -351,7 +451,7 @@
         tissue = jnp.where(label_of(x) != 0.0, 1.0, 0.0)
         ionic = ionic_gain * m * (m - ionic_onset) * (m - 1.0) + m * r
         mem_out[x] = m + TIME_STEP * (drive - tissue * ionic)
-    publish(3, halo0, NEXT, mem_out)
+    publish(2, halo0, NEXT, mem_out)
     for x in range(X0):
         m, r = mem[x], rec[x]
         rec_out[x] = r + TIME_STEP * recovery_rate * (-r - ionic_gain * m * (m - ionic_onset - 1.0))
@@ -391,7 +491,7 @@
             val, new = update(halo, slot, lambda x: src[x], c, b, x)
             dst[x] = jnp.where(halo.grid.colour(x, colour), new, val)
 
-    for x in inner_first(3, X0):
+    for x in inner_first(2, X0):
         m, near = halo0.neighbours(NEXT, lambda x: mem_out[x], x)
         rhs = jnp.zeros_like(m)
         for d in range(6):
@@ -399,30 +499,121 @@
         b0[x] = rhs * b0[x]
         val, new = update(halo0, V, lambda x: ext[x], c0, b0, x)
         va[x] = jnp.where(g0.colour(x, 0), new, val)
-    publish(4, halo0, RED, va)
+    publish(3, halo0, RED, va)
 
     first1 = (g1.lane == 0) & (iz == 0)
     last1 = (g1.lane == Z1 - 1) & (iz == nz - 1)
-    arrive(2)
-    for x in range(X1):
-        ci, ni = halo1.neighbours(INNER1, lambda x: in1[x], x, edge=True)
-        co, no = halo1.neighbours(OUTER1, lambda x: out1[x], x, edge=True)
-        full, diag, inv = scaled(g1, [jnp.minimum(ci, n) for n in ni], co, no, (first1, last1))
+    pack_row = lax.broadcasted_iota(jnp.int32, (RE, LANES), 0)
+    pack_lane = lax.broadcasted_iota(jnp.int32, (RE, LANES), 1)
+    pack_x = jnp.bitwise_and(pack_lane, XE - 1)
+    depth_parity = lax.div(pack_lane, XE) + iz + pack_x + pack_row
+    pack_own = [jnp.bitwise_and(depth_parity + colour, 1) == 0 for colour in range(2)]
+
+    def row_inside(row):
+        return (
+            (row < R1)
+            | ((row < R1 + GHOST) & (iy < ny - 1))
+            | ((row >= R1 + GHOST) & (iy > 0))
+        )
+
+    inside_row = row_inside(g1.row)
+    pack_inside = (
+        row_inside(pack_row)
+        & (pack_lane < GHOST * XE)
+        & ((pack_x >= GHOST) | (ix > 0))
+        & ((pack_x < X1 + GHOST) | (ix < nx - 1))
+    )
+
+    def inside1(p):
+        side = plane_side(p)
+        return inside_row if side is None else inside_row & side
+
+    def near1(planes, pack, p, edge=False):
+        val = planes(p)
+        side = jnp.broadcast_to(pack(p), (RE, Z1))
+        side_m, side_p = side, side
+        if edge:
+            side_m = jnp.where(iz == 0, 0.0, side)
+            side_p = jnp.where(iz == 0, side, 0.0)
+        return val, (
+            planes(p - 1),
+            planes(p + 1),
+            pltpu.roll(val, 1, 0),
+            pltpu.roll(val, RE - 1, 0),
+            jnp.where(g1.lane == 0, side_m, pltpu.roll(val, 1, 1)),
+            jnp.where(g1.lane == Z1 - 1, side_p, pltpu.roll(val, Z1 - 1, 1)),
+        )
+
+    def near_pack(planes, val, first, last):
+        own = jnp.zeros((RE, LANES), F32)
+        for p in range(first, last):
+            own = jnp.where(pack_lane == p, pltpu.roll(planes(p), p + 1 - iz, 1), own)
+        return (
+            pltpu.roll(val, 1, 1),
+            pltpu.roll(val, LANES - 1, 1),
+            pltpu.roll(val, 1, 0),
+            pltpu.roll(val, RE - 1, 0),
+            jnp.where(pack_lane < XE, own, pltpu.roll(val, XE, 1)),
+            pltpu.roll(val, LANES - XE, 1),
+        )
+
+    def scaled_wide(ci, ni, co, no, inside):
+        full = [jnp.minimum(ci, ni[k]) + 0.5 * (co + no[k]) for k in range(6)]
+        diag = ((full[0] + full[1]) + (full[2] + full[3])) + (full[4] + full[5])
+        inv = jnp.where(inside, 1.0 / diag, 0.0)
+        return [jnp.where(inside, f * inv, 0.0) for f in full], diag, inv
+
+    wide_arrive(0)
+    for p in range(1, XE - 1):
+        ci, ni = near1(lambda p: ee[INNER1, p], lambda p: zp1[INNER1, :, p : p + 1], p, edge=True)
+        co, no = near1(lambda p: ee[OUTER1, p], lambda p: zp1[OUTER1, :, p : p + 1], p, edge=True)
+        full, diag, inv = scaled_wide(ci, ni, co, no, inside1(p))
+        full[4] = jnp.where(first1, 0.0, full[4])
+        full[5] = jnp.where(last1, 0.0, full[5])
         for d in range(6):
-            c1[d, x] = full[d]
-        d1[x] = diag
-        b1[x] = inv
-
-    half_sweep(4, halo0, RED, va, vb, c0, b0, 1)
-    publish(5, halo0, BLACK, vb)
+            c1[d, p] = full[d]
+        if GHOST <= p < X1 + GHOST:
+            d1[p - GHOST] = diag[0:R1]
+            b1[p - GHOST] = inv[0:R1]
+    ci, co = zp1[INNER1], zp1[OUTER1]
+    full, _, _ = scaled_wide(
+        ci,
+        near_pack(lambda p: ee[INNER1, p], ci, 0, XE),
+        co,
+        near_pack(lambda p: ee[OUTER1, p], co, 0, XE),
+        pack_inside,
+    )
+    for d in range(6):
+        cz1[d] = full[d]
+
+    def stencil(b, c, near):
+        a = b + c(0) * near[0]
+        e = c(1) * near[1] + c(2) * near[2]
+        f = c(3) * near[3] + c(4) * near[4]
+        return (a + c(5) * near[5]) + (e + f)
+
+    def update1(src, pack, p):
+        val, near = near1(lambda p: src[p], lambda p: pack[:, p : p + 1], p)
+        return val, stencil(ee[RHS1, p], lambda d: c1[d, p], near)
+
+    def half1(src, pack, dst, colour, planes):
+        for p in planes:
+            val, new = update1(src, pack, p)
+            dst[p] = jnp.where(g1.colour(p, colour), new, val)
+
+    def half_pack(src, pack, dst, colour, first, last):
+        val = pack[...]
+        near = near_pack(lambda p: src[p], val, first, last)
+        new = stencil(zp1[RHS1], lambda d: cz1[d], near)
+        dst[...] = jnp.where(pack_own[colour], new, val)
+
+    half_sweep(3, halo0, RED, va, vb, c0, b0, 1)
+    publish(4, halo0, BLACK, vb)
 
     XG, RG, ZG = in2.shape
     XH, RH = XG // 2, RG // 2
     g2 = Grid(XG, RG, ZG)
     g3 = Grid(XH, RH, ZG)
-    tile_row = lax.broadcasted_iota(jnp.int32, (8, LANES), 0)
-    tile_lane = lax.broadcasted_iota(jnp.int32, (8, LANES), 1)
-
     def unpack(tile, dst):
         for px in range(nx):
             for py in range(ny // 2):
@@ -533,19 +724,27 @@
         val, new = update(halo0, BLACK, lambda x: vb[x], c0, b0, x)
         return d0[x] * (new - val)
 
-    for x, val in enumerate(restrict0(residual0, 0.5, 0, inner_first(5, X1))):
-        b1[x] = val * b1[x]
-        v1a[x] = jnp.where(g1.colour(x, 0), b1[x], 0.0)
-    publish(6, halo1, RED1, v1a)
-    half_sweep(6, halo1, RED1, v1a, v1b, c1, b1, 1)
-    publish(7, halo1, BLACK1, v1b)
+    for x, val in enumerate(restrict0(residual0, 0.5, 0, inner_first(4, X1))):
+        ee[RHS1, GHOST + x, 0:R1, :] = val * b1[x]
+    wide_publish(1)
+    wide_arrive(1)
+    ring = GHOST - 1
+    for p in range(ring - 1, XE - ring + 1):
+        v1a[p] = jnp.where(g1.colour(p, 0), ee[RHS1, p], 0.0)
+    z1a[...] = jnp.where(pack_own[0], zp1[RHS1], 0.0)
+    half_pack(v1a, z1a, z1b, 1, ring, XE - ring)
+    half1(v1a, z1a, v1b, 1, range(ring, XE - ring))
 
     def residual1(x):
-        val, new = update(halo1, BLACK1, lambda x: v1b[x], c1, b1, x)
-        return d1[x] * (new - val)
-
-    gr_own[...] = restrict1(residual1, 0.5, inner_first(7, X2))
+        val, new = update1(v1b, z1b, GHOST + x)
+        return d1[x] * (new - val)[0:R1]
+
+    gr_own[...] = restrict1(residual1, 0.5)
     gather_send(gr_own, gr, 1)
+    for p in (0, 1, XE - 2, XE - 1):
+        v1a[p] = jnp.where(g1.colour(p, 0), ee[RHS1, p], 0.0)
+    half_pack(v1a, z1a, z1b, 1, 0, XE)
+    half1(v1a, z1a, v1b, 1, (1, 2, XE - 3, XE - 2))
     gather_wait(gr, 1, True)
     unpack(lambda t: gr[t], v2b)
     for x in range(XG):
@@ -603,43 +802,36 @@
 
     row_shift = lax.rem(RG - iy * R2, RG)
     lane_shift = lax.rem(ZG - iz * half, ZG)
-    lane8 = lax.broadcasted_iota(jnp.int32, (8, LANES), 1)
-    side = jnp.zeros((8, LANES), F32)
-    below, above = X2 * 8, X2 * 8 + 8
-    low, high, across = above + 8, above + 16, above + 24
-    tall[low : across, 0:ZG] = jnp.zeros((across - low, ZG), F32)
-    for k in range(-1, X2 + 1):
-        part = v2a[jnp.clip(ix * X2 + k, 0, XG - 1)]
+    edge2 = GHOST // 2
+    rows2 = R2 + 2 * edge2
+    planes2 = X2 + 2 * edge2
+    for k in range(planes2):
+        part = v2a[jnp.clip(ix * X2 + k - edge2, 0, XG - 1)]
         part = pltpu.roll(pltpu.roll(part, row_shift, 0), lane_shift, 1)
-        if k < 0:
-            tall[below : below + 8, 0:ZG] = jnp.where(ix > 0, part[0:8], 0.0)
-        elif k == X2:
-            tall[above : above + 8, 0:ZG] = jnp.where(ix < nx - 1, part[0:8], 0.0)
-        else:
-            tall[k * 8 : (k + 1) * 8, 0:ZG] = part[0:8]
-            tall[low + k : low + k + 1, 0:ZG] = jnp.where(iy > 0, part[RG - 1 : RG], 0.0)
-            tall[high + k : high + k + 1, 0:ZG] = jnp.where(iy < ny - 1, part[R2 : R2 + 1], 0.0)
-            turned = pltpu.roll(part[0:8], k + 1 + (half - 1) * (1 - iz), 1)
-            side = jnp.where(lane8 == k, turned, side)
-    tall[across : across + 8, 0:ZG] = side
-    wide = dot(tall[0 : across + 8, 0:ZG], double12)
-
-    def grown(slot, row):
-        return double_rows(tmp, slot, wide[row : row + R2])
-
-    for x in range(X2):
-        corr = grown(x, x * 8)
-        v1a[2 * x] = v1b[2 * x] + corr
-        v1a[2 * x + 1] = v1b[2 * x + 1] + corr
-    xh1[0, FIXED1] = xh1[0, BLACK1] + grown(0, below)
-    xh1[1, FIXED1] = xh1[1, BLACK1] + grown(1, above)
-    yh1[0, FIXED1] = yh1[0, BLACK1] + grown(2, low)
-    yh1[1, FIXED1] = yh1[1, BLACK1] + grown(3, high)
-    zh1[FIXED1] = zh1[BLACK1] + grown(0, across)
-    half_sweep(None, halo1, FIXED1, v1a, v1b, c1, b1, 0)
-    publish(8, halo1, LASTRED1, v1b)
-    half_sweep(8, halo1, LASTRED1, v1b, v1a, c1, b1, 1)
-    publish(9, halo1, LASTBLACK1, v1a)
+        tall[k * rows2 : (k + 1) * rows2, 0:ZG] = jnp.where(
+            tile_row < R2 + edge2, part[0:rows2], part[RG - rows2 : RG]
+        )
+    source = lax.broadcasted_iota(jnp.int32, (ZG, LANES), 0)
+    target = lax.broadcasted_iota(jnp.int32, (ZG, LANES), 1)
+    target = lax.div(target, 2 * XE)
+    pick = jnp.where(source == jnp.where(iz == 0, half + target, ZG - 1 - target), 1.0, 0.0).astype(F32)
+    coarse_rows = tall[0 : planes2 * rows2, 0:ZG]
+    wide = dot(coarse_rows, double12)
+    sides = dot(coarse_rows, pick)
+    acc = jnp.zeros((rows2, LANES), F32)
+    tile_plane = lax.div(jnp.bitwise_and(tile_lane, XE - 1), 2)
+    for k in range(planes2):
+        acc = jnp.where(tile_plane == k, sides[k * rows2 : (k + 1) * rows2], acc)
+    z1a[...] = z1b[...] + jnp.where(pack_inside, double_rows(tmp, 0, acc), 0.0)
+    for k in range(planes2):
+        corr = double_rows(tmp, k, wide[k * rows2 : (k + 1) * rows2])
+        for p in (2 * k, 2 * k + 1):
+            if 0 < p < XE - 1:
+                v1a[p] = v1b[p] + jnp.where(inside1(p), corr, 0.0)
+    half_pack(v1a, z1a, z1b, 0, 1, XE - 1)
+    half1(v1a, z1a, v1b, 0, range(2, XE - 2))
+    half_pack(v1b, z1b, z1a, 1, 2, XE - 2)
+    half1(v1b, z1b, v1a, 1, range(3, XE - 3))
 
     def enlarge(count, read, write):
         for x in range(count):
@@ -652,15 +844,17 @@
         va[2 * x] = vb[2 * x] + corr
         va[2 * x + 1] = vb[2 * x + 1] + corr
 
-    enlarge(X1, lambda x: v1a[x], inside)
-    arrive(9)
+    enlarge(X1, lambda x: v1a[GHOST + x, 0:R1, :], inside)
+    for x in range(X1):
+        yrim[0, x : x + 1, :] = v1a[GHOST + x, RE - 1 : RE, :]
+        yrim[1, x : x + 1, :] = v1a[GHOST + x, R1 : R1 + 1, :]
 
     def rim(k):
         if k < 2:
-            return xh1[k, LASTBLACK1]
+            return v1a[GHOST - 1 if k == 0 else X1 + GHOST, 0:R1, :]
         if k < 4:
-            return yh1[k - 2, LASTBLACK1]
-        return zh1[LASTBLACK1]
+            return yrim[k - 2]
+        return pltpu.roll(z1a[0:R1, :], LANES - GHOST, 1)
 
     def outside(k, corr):
         if k < 2:
@@ -672,11 +866,13 @@
 
     enlarge(5, rim, outside)
     half_sweep(None, halo0, FIXED, va, vb, c0, b0, 0)
-    publish(10, halo0, LAST, vb)
-    half_sweep(10, halo0, LAST, vb, ext_out, c0, b0, 1)
+    publish(5, halo0, LAST, vb)
+    half_sweep(5, halo0, LAST, vb, ext_out, c0, b0, 1)
 
     for number in range(len(EXCHANGES)):
         sent(number)
+    for number in range(len(WIDE)):
+        wide_sent(number)
     gather_wait(gc, 0, False)
     gather_wait(gr, 1, False)
 
@@ -702,7 +898,7 @@
         assert nz == 2 and ny % 2 == 0 and ZG == LANES and Z1 == LANES
         assert R1 == 8 and X1 == 8 and X % 8 == 0
         total = nx * ny * nz
-        f0, f1 = 9, 7
+        f0 = 9
         field = (X, R, Z)
         lvl1 = (X1, R1, Z1)
         whole = (XG, RG, ZG)
@@ -716,21 +912,28 @@
 
         anywhere = pl.BlockSpec(memory_space=pl.ANY)
         scratch = [v(*field)] * 4 + [pltpu.VMEM(labels.shape, jnp.int32), pltpu.SemaphoreType.DMA((5,))]
-        scratch += faces(f0, *field) + faces(f1, *lvl1)
+        scratch += faces(f0, *field)
         scratch += [v(*field), v(*field), v(*field), v(6, *field), v(6, *field), v(*field), v(*field)]
         scratch += [v(*field), v(*field)]
         scratch += [
             v(2 * max(X1, XG // 2), max(R, RG), LANES),
             v(max(X1 * R1, (XG // 2) * (RG // 2), 2 * X1 * R1), Z),
         ]
-        scratch += [v(*lvl1), v(*lvl1), v(6, *lvl1), v(*lvl1), v(*lvl1), v(*lvl1), v(*lvl1)]
+        XE, RE = X1 + 2 * GHOST, R1 + 2 * GHOST
+        assert GHOST * XE <= LANES and 2 * GHOST == R1 and GHOST <= X1
+        wide, pack = (XE, RE, Z1), (RE, LANES)
+        scratch += [v(3, *wide), v(2, 3, X1 // 2, R1, Z1), v(2, 3, XE // 2, R1, Z1), v(3, R1, LANES)]
+        scratch += [v(9, 3, R1, LANES), v(3, *pack), v(6, *wide), v(6, *pack), v(*lvl1), v(*lvl1)]
+        scratch += [v(*wide), v(*wide), v(*pack), v(*pack), v(2, X1, Z1)]
         scratch += [v(2, 8, LANES), v(total, 2, 8, LANES), v(8, LANES), v(total, 8, LANES)]
         scratch += [v(*whole), v(*whole), v(6, *whole), v(*whole), v(*whole), v(*whole), v(*whole)]
         scratch += [v(6, *third), v(*third), v(*third)]
         packed = (XG // 4, RG // 2, ZG)
         scratch += [v(12, *packed), v(2, *packed)]
         sems = SIDES * len(EXCHANGES)
-        scratch += [pltpu.SemaphoreType.DMA((sems,))] * 2 + [pltpu.SemaphoreType.DMA((2,))] * 2
+        scratch += [pltpu.SemaphoreType.DMA((sems,))] * 2
+        scratch += [pltpu.SemaphoreType.DMA((WIDE_SIDES * len(WIDE),))] * 2
+        scratch += [pltpu.SemaphoreType.DMA((2,))] * 2
         vmem = pl.BlockSpec(memory_space=pltpu.VMEM)
         room = 54400 << 10
         shape = jax.ShapeDtypeStruct(field, F32)

time: 50.6 us -> 46 us (0.909)
  Pallas kernels: 49.1 us -> 44.5 us
    pallas_call x1, Pallas kernels: 48.2 us -> 43.6 us  [on_device(): pl.pallas_call(functools.partial(kernel, (nx, ny, nz)), out_shape=[shape]...]
where the time goes in v2:
time: 46 us; the launch traced here: 45.9 us
  Pallas kernels  44.5 us (97%)
  local copies, waits for them, and re-layouts  0.67 us (1%)
  between operations  0.65 us (1%)
    pallas_call x1, Pallas kernels, on_device(): pl.pallas_call(functools.partial(kernel, (nx, ny, nz)), out_shape=[shape]...  43.6 us

profile of v2, /device:TPU:0, one launch (start us, length us, event | category | flops | bytes accessed | tf_op | source)
XLA Modules:
  0.0 45.9 jit_solution(4677562110609931459)
XLA Ops:
  0.6 0.0 copy-start
  0.6 0.7 %copy-done = s32[2,2,32]{2,1,0:T(2,128)S(1)} copy-done((s32[2,2,32]{2,1,0:T(2,128)S(1)}, s32[2,2,32]{2,1,0:T(2,128)}, u32[]{:S(2)}) %copy-start) | copy-done | bytes 536
  1.3 43.6 %shard_map.76 = (f32[16,16,256]{2,1,0:T(8,128)S(1)}, f32[16,16,256]{2,1,0:T(8,128)S(1)}, f32[16,16,256]{2,1,0:T(8,128)S(1)}) custom-call(f32[16,16,256]{2,1,0:T(8,128)} %refs_0_.1, f32[16,16,256]{2,1,0:T(8,128)} %refs_1_.1, f32[16,16,256]{2,1,0:T(8,128)} %refs_2_.1, f32[16,16,256]{2,1,0:T(8,128)} %refs_3_.1, s32[2,2,32]{2,1,0:T(2,128)S(1)} %copy-done), custom_call_target="tpu_custom_call" | custom-call | tf_op jit(solution)/shard_map/pallas_call | solution.py:940
  45.0 0.9 %shard_map.77 = (f32[16,16,256]{2,1,0:T(8,128)}, f32[16,16,256]{2,1,0:T(8,128)}, f32[16,16,256]{2,1,0:T(8,128)}) custom-call(f32[16,16,256]{2,1,0:T(8,128)S(1)} %get-tuple-element.6.refs_0_, f32[16,16,256]{2,1,0:T(8,128)S(1)} %get-tuple-element.7.refs_1_, f32[16,16,256]{2,1,0:T(8,128)S(1)} %get-tuple-element.8.refs_2_), custom_call_target="tpu_custom_call" | custom-call | tf_op jit(solution)/shard_map/pallas_call | solution.py:951
Async XLA Ops:
  0.6 0.7 %copy-start = (s32[2,2,32]{2,1,0:T(2,128)S(1)}, s32[2,2,32]{2,1,0:T(2,128)}, u32[]{:S(2)}) copy-start(s32[2,2,32]{2,1,0:T(2,128)} %refs_4_.1) | copy-start | bytes 1540

commit v3 on v2

--- a/solution.py
+++ b/solution.py
@@ -13,6 +13,7 @@
 ionic_onset = 0.15
 recovery_rate = 0.01
 MESH = pl.DeviceIdType.MESH
+LOGICAL = pl.DeviceIdType.LOGICAL
 LANES = 128
 F32 = jnp.float32
 
@@ -28,7 +29,7 @@
     (LAST, 1),
 )
 SIDES = 5
-WIDE = ((INNER1, 2), (RHS1, 1))
+WIDE = ((INNER1, 1), (RHS1, 1))
 STEPS = (-1, 0, 1)
 WIDE_SIDES = 17
 
@@ -143,8 +144,8 @@
     (xs0, ys0, zs0, xh0, yh0, zh0) = refs[7:13]
     (in0, out0, uu, w0, c0, d0, b0, va, vb, tmp, tall) = refs[13:24]
     (ee, ys1, yr1, zs1, zr1, zp1, c1, cz1, d1, b1, v1a, v1b, z1a, z1b, yrim) = refs[24:39]
-    (gc_own, gc, gr_own, gr, in2, out2, c2, d2, b2, v2a, v2b) = refs[39:50]
-    (c3, b3, v3, k3, h3, send_sem, recv_sem, wide_send, wide_recv, gs_sem, gr_sem) = refs[50:]
+    (lab_own, lab_all, gc_own, gc, gr_own, gr, in2, out2, c2, d2, b2, v2a, v2b) = refs[39:52]
+    (c3, b3, v3, k3, h3, send_sem, recv_sem, wide_send, wide_recv, gs_sem, gr_sem) = refs[52:]
     nx, ny, nz = counts
     ix, iy, iz = lax.axis_index("gx"), lax.axis_index("gy"), lax.axis_index("gz")
     me = (ix * ny + iy) * nz + iz
@@ -160,14 +161,11 @@
     barrier = pltpu.get_barrier_semaphore()
 
     def others(body):
-        def step(i, carry):
-            dev = lax.rem(me + i, total)
-            body(dev, (dev // (ny * nz), lax.rem(dev // nz, ny), lax.rem(dev, nz)))
-            return carry
-
-        lax.fori_loop(1, total, step, 0)
-
-    others(lambda dev, where: pl.semaphore_signal(barrier, inc=1, device_id=where, device_id_type=MESH))
+        for i in range(1, total):
+            dev = me + i
+            body(jnp.where(dev >= total, dev - total, dev))
+
+    others(lambda dev: pl.semaphore_signal(barrier, inc=1, device_id=dev, device_id_type=LOGICAL))
 
     def clear(missing, ref, side):
         def fill():
@@ -351,14 +349,14 @@
             maybe(goes, copy.wait_send)
 
     def gather_send(own, whole, which):
-        def go(dev, where):
+        def go(dev):
             pltpu.make_async_remote_copy(
                 src_ref=own,
                 dst_ref=whole.at[me],
                 send_sem=gs_sem.at[which],
                 recv_sem=gr_sem.at[which],
-                device_id=where,
-                device_id_type=MESH,
+                device_id=dev,
+                device_id_type=LOGICAL,
             ).start()
 
         others(go)
@@ -394,6 +392,12 @@
             )
         )
 
+    spread = copy_matrix(lab.shape[2], LANES, 0)
+
+    def lab_lane(bx, by, at):
+        line = jnp.dot(lab[bx].astype(F32), spread, preferred_element_type=F32)[by : by + 1]
+        return jnp.broadcast_to(pltpu.roll(jnp.broadcast_to(line, (8, LANES)), at * lab.shape[2], 1), (8, LANES))
+
     def label_of(x):
         return lab_planes[x // 8]
 
@@ -402,10 +406,17 @@
         in0[x] = jnp.where(label == 1.0, 1.0, jnp.where(label == 2.0, 0.3, 0.0)) * fib[x]
         out0[x] = jnp.where(label == 0.0, 3.0, 1.0)
         uu[x] = mem[x] + ext[x]
+    acc = jnp.zeros((8, LANES), F32)
+    for bx in range(lab.shape[0]):
+        for by in range(lab.shape[1]):
+            at = bx * lab.shape[1] + by
+            acc = jnp.where(lax.shift_right_logical(tile_lane, 5) == at, lab_lane(bx, by, at), acc)
+    lab_own[...] = acc[0:1]
     halo0.put(INNER, in0)
     halo0.put(U, uu)
     pl.semaphore_wait(barrier, total - 1)
     send(0)
+    gather_send(lab_own, lab_all, 2)
     halo0.put(OUTER, out0)
     halo0.put(V, ext)
     send(1)
@@ -429,15 +440,6 @@
         low = jnp.concatenate(rows[: X2 // 2], axis=0)
         high = jnp.concatenate(rows[X2 // 2 :], axis=0)
         return (dot(low, narrow_low) + dot(high, narrow_high)) * factor
-
-    for x, val in enumerate(restrict0(lambda x: in0[x], 0.125, 0)):
-        ee[INNER1, GHOST + x, 0:R1, :] = val
-    for x, val in enumerate(restrict0(lambda x: out0[x], 0.125, 0)):
-        ee[OUTER1, GHOST + x, 0:R1, :] = val
-    wide_publish(0)
-    gc_own[0] = restrict1(lambda x: ee[INNER1, GHOST + x, 0:R1, :], 0.125)
-    gc_own[1] = restrict1(lambda x: ee[OUTER1, GHOST + x, 0:R1, :], 0.125)
-    gather_send(gc_own, gc, 0)
 
     for x in inner_first(0, X0):
         centre, near = halo0.neighbours(INNER, lambda x: in0[x], x, edge=True)
@@ -456,6 +458,11 @@
         m, r = mem[x], rec[x]
         rec_out[x] = r + TIME_STEP * recovery_rate * (-r - ionic_gain * m * (m - ionic_onset - 1.0))
 
+    for x, val in enumerate(restrict0(lambda x: in0[x], 0.125, 0)):
+        ee[INNER1, GHOST + x, 0:R1, :] = val
+    wide_publish(0)
+    gc_own[...] = restrict1(lambda x: ee[INNER1, GHOST + x, 0:R1, :], 0.125)
+
     def scaled(grid, weights, centre, near, iz_edges):
         full = [weights[d] + 0.5 * (centre + near[d]) for d in range(6)]
         diag = ((full[0] + full[1]) + (full[2] + full[3])) + (full[4] + full[5])
@@ -500,6 +507,7 @@
         val, new = update(halo0, V, lambda x: ext[x], c0, b0, x)
         va[x] = jnp.where(g0.colour(x, 0), new, val)
     publish(3, halo0, RED, va)
+    gather_send(gc_own, gc, 0)
 
     first1 = (g1.lane == 0) & (iz == 0)
     last1 = (g1.lane == Z1 - 1) & (iz == nz - 1)
@@ -563,6 +571,49 @@
         inv = jnp.where(inside, 1.0 / diag, 0.0)
         return [jnp.where(inside, f * inv, 0.0) for f in full], diag, inv
 
+    gather_wait(lab_all, 2, True)
+    blocks = [(sx, bx) for sx, bx in ((-1, 1), (0, 0), (0, 1), (1, 0))]
+    lines = [(0, 0), (0, 1), (1, 0), (-1, 1)]
+    span = lab.shape[2]
+    for z in range(2):
+        core = iz if z == 0 else 1 - iz
+        for i, (sx, bx) in enumerate(blocks):
+            for j, (sy, by) in enumerate(lines):
+                px, py = jnp.clip(ix + sx, 0, nx - 1), jnp.clip(iy + sy, 0, ny - 1)
+                at = (z * 4 + i) * 4 + j
+                tall[at : at + 1, 0:LANES] = lab_all[(px * ny + py) * nz + core]
+    near_labels = tall[0:32, 0:LANES]
+    order = lax.bitwise_and(lax.broadcasted_iota(jnp.int32, (32, LANES), 0), 15)
+    segment = jnp.zeros((32, LANES), jnp.int32)
+    for i, (_, bx) in enumerate(blocks):
+        for j, (_, by) in enumerate(lines):
+            segment = jnp.where(order == i * 4 + j, bx * lab.shape[1] + by, segment)
+    lined = near_labels
+    for k in range(1, LANES // span):
+        lined = jnp.where(segment == k, pltpu.roll(near_labels, LANES - k * span, 1), lined)
+    stretched = jnp.dot(lined[0:16], copy_matrix(LANES, Z1, 2), preferred_element_type=F32)
+    edge_labels = jnp.where(iz == 0, lined[16:32, 0:1], lined[16:32, span - 1 : span])
+    edge_labels = jnp.broadcast_to(edge_labels, (16, LANES))
+    group = lax.shift_right_logical(g1.row, 2)
+    pack_group = lax.shift_right_logical(pack_row, 2)
+    pack_block = lax.shift_right_logical(pack_x, 2)
+    packed_labels = jnp.zeros((RE, LANES), F32)
+    for i in range(4):
+        block_labels = jnp.zeros((RE, Z1), F32)
+        for j in range(4):
+            at = i * 4 + j
+            block_labels = jnp.where(
+                group == j, jnp.broadcast_to(stretched[at : at + 1], (RE, Z1)), block_labels
+            )
+            packed_labels = jnp.where(
+                (pack_group == j) & (pack_block == i),
+                jnp.broadcast_to(edge_labels[at : at + 1], (RE, LANES)),
+                packed_labels,
+            )
+        block_outer = jnp.where(block_labels == 0.0, 3.0, 1.0)
+        for p in range(4 * i, 4 * i + 4):
+            ee[OUTER1, p] = jnp.where(inside1(p), block_outer, 0.0)
+    zp1[OUTER1] = jnp.where(pack_inside, jnp.where(packed_labels == 0.0, 3.0, 1.0), 0.0)
     wide_arrive(0)
     for p in range(1, XE - 1):
         ci, ni = near1(lambda p: ee[INNER1, p], lambda p: zp1[INNER1, :, p : p + 1], p, edge=True)
@@ -697,8 +748,27 @@
         return [whole[x * RH : (x + 1) * RH] for x in range(XH)]
 
     gather_wait(gc, 0, True)
-    unpack(lambda t: gc[t, 0], in2)
-    unpack(lambda t: gc[t, 1], out2)
+    unpack(lambda t: gc[t], in2)
+    for t in range(total):
+        tall[t : t + 1, 0:LANES] = lab_all[t]
+    k = lax.broadcasted_iota(jnp.int32, (LANES, LANES), 0)
+    j = lax.broadcasted_iota(jnp.int32, (LANES, LANES), 1)
+    from_lane = lax.div(j, half) * (lab.shape[1] * span) + lax.div(lax.rem(j, half), half // span)
+    every = [
+        jnp.dot(
+            tall[0:total, 0:LANES],
+            jnp.where(k == from_lane + by * span, 1.0, 0.0).astype(F32),
+            preferred_element_type=F32,
+        )
+        for by in range(2)
+    ]
+    first_rows = lax.rem(tile_row, R2) < R2 // 2
+
+    def label_tile(t):
+        pair = [jnp.broadcast_to(e[t : t + 1], (8, LANES)) for e in every]
+        return jnp.where(jnp.where(first_rows, pair[0], pair[1]) == 0.0, 3.0, 1.0)
+
+    unpack(label_tile, out2)
     whole_couplings(g2, in2, out2, ZG - 1, c2, d2, b2)
     for x, val in enumerate(restrict2(lambda x: in2[x], 0.125)):
         v3[x] = val
@@ -875,6 +945,7 @@
         wide_sent(number)
     gather_wait(gc, 0, False)
     gather_wait(gr, 1, False)
+    gather_wait(lab_all, 2, False)
 
 
 def finish(*refs):
@@ -898,6 +969,7 @@
         assert nz == 2 and ny % 2 == 0 and ZG == LANES and Z1 == LANES
         assert R1 == 8 and X1 == 8 and X % 8 == 0
         total = nx * ny * nz
+        assert labels.shape == (2, 2, LANES // 4)
         f0 = 9
         field = (X, R, Z)
         lvl1 = (X1, R1, Z1)
@@ -917,7 +989,7 @@
         scratch += [v(*field), v(*field)]
         scratch += [
             v(2 * max(X1, XG // 2), max(R, RG), LANES),
-            v(max(X1 * R1, (XG // 2) * (RG // 2), 2 * X1 * R1), Z),
+            v(max(X1 * R1, (XG // 2) * (RG // 2), 2 * X1 * R1, total), Z),
         ]
         XE, RE = X1 + 2 * GHOST, R1 + 2 * GHOST
         assert GHOST * XE <= LANES and 2 * GHOST == R1 and GHOST <= X1
@@ -925,7 +997,7 @@
         scratch += [v(3, *wide), v(2, 3, X1 // 2, R1, Z1), v(2, 3, XE // 2, R1, Z1), v(3, R1, LANES)]
         scratch += [v(9, 3, R1, LANES), v(3, *pack), v(6, *wide), v(6, *pack), v(*lvl1), v(*lvl1)]
         scratch += [v(*wide), v(*wide), v(*pack), v(*pack), v(2, X1, Z1)]
-        scratch += [v(2, 8, LANES), v(total, 2, 8, LANES), v(8, LANES), v(total, 8, LANES)]
+        scratch += [v(1, LANES), v(total, 1, LANES), v(8, LANES), v(total, 8, LANES), v(8, LANES), v(total, 8, LANES)]
         scratch += [v(*whole), v(*whole), v(6, *whole), v(*whole), v(*whole), v(*whole), v(*whole)]
         scratch += [v(6, *third), v(*third), v(*third)]
         packed = (XG // 4, RG // 2, ZG)
@@ -933,7 +1005,7 @@
         sems = SIDES * len(EXCHANGES)
         scratch += [pltpu.SemaphoreType.DMA((sems,))] * 2
         scratch += [pltpu.SemaphoreType.DMA((WIDE_SIDES * len(WIDE),))] * 2
-        scratch += [pltpu.SemaphoreType.DMA((2,))] * 2
+        scratch += [pltpu.SemaphoreType.DMA((3,))] * 2
         vmem = pl.BlockSpec(memory_space=pltpu.VMEM)
         room = 54400 << 10
         shape = jax.ShapeDtypeStruct(field, F32)

time: 46 us -> 41.7 us (0.907)
  Pallas kernels: 44.5 us -> 40.3 us
    pallas_call x1, Pallas kernels: 43.6 us -> 39.3 us  [on_device(): pl.pallas_call(functools.partial(kernel, (nx, ny, nz)), out_shape=[shape]...]
where the time goes in v3:
time: 41.7 us; the launch traced here: 41.6 us
  Pallas kernels  40.3 us (97%)
  local copies, waits for them, and re-layouts  0.67 us (2%)
  between operations  0.65 us (2%)
    pallas_call x1, Pallas kernels, on_device(): pl.pallas_call(functools.partial(kernel, (nx, ny, nz)), out_shape=[shape]...  39.3 us
    pallas_call x1, Pallas kernels, on_device(): pl.pallas_call(finish, out_shape=[shape] * 3, in_specs=[vmem] * 3, out_sp...  0.9 us

profile of v3, /device:TPU:0, one launch (start us, length us, event | category | flops | bytes accessed | tf_op | source)
XLA Modules:
  0.0 41.6 jit_solution(12157473935526797438)
XLA Ops:
  0.6 0.0 copy-start
  0.6 0.7 %copy-done = s32[2,2,32]{2,1,0:T(2,128)S(1)} copy-done((s32[2,2,32]{2,1,0:T(2,128)S(1)}, s32[2,2,32]{2,1,0:T(2,128)}, u32[]{:S(2)}) %copy-start) | copy-done | bytes 536
  1.3 39.3 %shard_map.76 = (f32[16,16,256]{2,1,0:T(8,128)S(1)}, f32[16,16,256]{2,1,0:T(8,128)S(1)}, f32[16,16,256]{2,1,0:T(8,128)S(1)}) custom-call(f32[16,16,256]{2,1,0:T(8,128)} %refs_0_.1, f32[16,16,256]{2,1,0:T(8,128)} %refs_1_.1, f32[16,16,256]{2,1,0:T(8,128)} %refs_2_.1, f32[16,16,256]{2,1,0:T(8,128)} %refs_3_.1, s32[2,2,32]{2,1,0:T(2,128)S(1)} %copy-done), custom_call_target="tpu_custom_call" | custom-call | tf_op jit(solution)/shard_map/pallas_call | solution.py:1012
  40.7 0.9 %shard_map.77 = (f32[16,16,256]{2,1,0:T(8,128)}, f32[16,16,256]{2,1,0:T(8,128)}, f32[16,16,256]{2,1,0:T(8,128)}) custom-call(f32[16,16,256]{2,1,0:T(8,128)S(1)} %get-tuple-element.6.refs_0_, f32[16,16,256]{2,1,0:T(8,128)S(1)} %get-tuple-element.7.refs_1_, f32[16,16,256]{2,1,0:T(8,128)S(1)} %get-tuple-element.8.refs_2_), custom_call_target="tpu_custom_call" | custom-call | tf_op jit(solution)/shard_map/pallas_call | solution.py:1023
Async XLA Ops:
  0.6 0.7 %copy-start = (s32[2,2,32]{2,1,0:T(2,128)S(1)}, s32[2,2,32]{2,1,0:T(2,128)}, u32[]{:S(2)}) copy-start(s32[2,2,32]{2,1,0:T(2,128)} %refs_4_.1) | copy-start | bytes 1540

commit v4 on v3

--- a/solution.py
+++ b/solution.py
@@ -17,7 +17,7 @@
 LANES = 128
 F32 = jnp.float32
 
-INNER, U, OUTER, V, NEXT, RED, BLACK, FIXED, LAST = range(9)
+INNER, U, OUTER, V, NEXT, RED, BLACK, MIXED, READY, FIXED, LAST = range(11)
 INNER1, OUTER1, RHS1 = range(3)
 GHOST = 4
 EXCHANGES = (
@@ -26,7 +26,7 @@
     (NEXT, 1),
     (RED, 1),
     (BLACK, 1),
-    (LAST, 1),
+    (MIXED, 2),
 )
 SIDES = 5
 WIDE = ((INNER1, 1), (RHS1, 1))
@@ -143,9 +143,9 @@
     refs = (None,) + refs
     (xs0, ys0, zs0, xh0, yh0, zh0) = refs[7:13]
     (in0, out0, uu, w0, c0, d0, b0, va, vb, tmp, tall) = refs[13:24]
-    (ee, ys1, yr1, zs1, zr1, zp1, c1, cz1, d1, b1, v1a, v1b, z1a, z1b, yrim) = refs[24:39]
-    (lab_own, lab_all, gc_own, gc, gr_own, gr, in2, out2, c2, d2, b2, v2a, v2b) = refs[39:52]
-    (c3, b3, v3, k3, h3, send_sem, recv_sem, wide_send, wide_recv, gs_sem, gr_sem) = refs[52:]
+    (ee, ys1, yr1, zs1, zr1, zp1, c1, cz1, d1, b1, v1a, v1b, z1a, z1b, yrim, mixed, tall2) = refs[24:41]
+    (lab_own, lab_all, gc_own, gc, gr_own, gr, in2, out2, c2, d2, b2, v2a, v2b) = refs[41:54]
+    (c3, b3, v3, k3, h3, send_sem, recv_sem, wide_send, wide_recv, gs_sem, gr_sem) = refs[54:]
     nx, ny, nz = counts
     ix, iy, iz = lax.axis_index("gx"), lax.axis_index("gy"), lax.axis_index("gz")
     me = (ix * ny + iy) * nz + iz
@@ -469,21 +469,25 @@
         inv = 1.0 / diag
         full = [f * inv for f in full]
         low, high = iz_edges
+        along_z = jnp.where(even_lane, full[4], full[5])
         full[4] = jnp.where(low, 0.0, full[4])
         full[5] = jnp.where(high, 0.0, full[5])
-        return full, diag, inv
-
+        return full, diag, inv, along_z
+
+    even_lane = jnp.bitwise_and(g0.lane, 1) == 0
+    even_row = jnp.bitwise_and(g0.row, 1) == 0
     first0 = (g0.lane == 0) & (iz == 0)
     last0 = (g0.lane == Z0 - 1) & (iz == nz - 1)
     arrive(1)
     inv0 = vb
     for x in range(X0):
         centre, near = halo0.neighbours(OUTER, lambda x: out0[x], x, edge=True)
-        full, diag, inv = scaled(g0, [w0[d, x] for d in range(6)], centre, near, (first0, last0))
+        full, diag, inv, along_z = scaled(g0, [w0[d, x] for d in range(6)], centre, near, (first0, last0))
         for d in range(6):
             c0[d, x] = full[d]
         d0[x] = diag
         b0[x] = inv
+        mixed[x] = pltpu.roll(along_z, 1, 1)
 
     def update(halo, slot, planes, c, b, x):
         val, near = halo.neighbours(slot, planes, x)
@@ -747,6 +751,37 @@
         whole = dot(tall[0 : XH * RH, 0:ZG], narrow_low) * factor
         return [whole[x * RH : (x + 1) * RH] for x in range(XH)]
 
+    def mix(x, a, b):
+        return jnp.where(g0.colour(x, 0), a, pltpu.roll(b, 1, 1))
+
+    across = jnp.zeros((R0, LANES), F32)
+    face_lane = lax.broadcasted_iota(jnp.int32, (R0, LANES), 1)
+    for x in range(X0):
+        along_y = jnp.where(even_row, c0[2, x], c0[3, x])
+        along_x = c0[x % 2, x]
+        if x == 0 or x == X0 - 1:
+            xs0[x // (X0 - 1), MIXED] = mix(x, c0[x % 2, x], along_y)
+        val = mix(x, jnp.where(g0.row < R0 // 2, c0[2, x], c0[3, x]), along_x)
+        ys0[0, MIXED, x : x + 1, :] = val[0:1]
+        ys0[1, MIXED, x : x + 1, :] = val[R0 - 1 :]
+        toward = jnp.where(iz == 0, c0[5, x, :, Z0 - LANES :], c0[4, x, :, 0:LANES])
+        outs = [toward] + [
+            jnp.where(iz == 0, f[:, Z0 - LANES :], f[:, 0:LANES]) for f in (along_x, along_y)
+        ]
+        for k, end in enumerate(outs):
+            at = k * X0 + x
+            across = jnp.where(face_lane == at, pltpu.roll(end, at + 1 - iz, 1), across)
+    zs0[MIXED] = across
+    def residual0(x):
+        val, new = update(halo0, BLACK, lambda x: vb[x], c0, b0, x)
+        mixed[x] = jnp.where(g0.colour(x, 0), new, mixed[x])
+        return d0[x] * (new - val)
+
+    for x, val in enumerate(restrict0(residual0, 0.5, 0, inner_first(4, X1))):
+        ee[RHS1, GHOST + x, 0:R1, :] = val * b1[x]
+    wide_publish(1)
+    halo0.put(READY, mixed)
+    send(5)
     gather_wait(gc, 0, True)
     unpack(lambda t: gc[t], in2)
     for t in range(total):
@@ -790,13 +825,6 @@
             for k in range(2, 6):
                 k3[colour * 6 + k, p] = pack(colour, c3[k, a], c3[k, z])
 
-    def residual0(x):
-        val, new = update(halo0, BLACK, lambda x: vb[x], c0, b0, x)
-        return d0[x] * (new - val)
-
-    for x, val in enumerate(restrict0(residual0, 0.5, 0, inner_first(4, X1))):
-        ee[RHS1, GHOST + x, 0:R1, :] = val * b1[x]
-    wide_publish(1)
     wide_arrive(1)
     ring = GHOST - 1
     for p in range(ring - 1, XE - ring + 1):
@@ -915,29 +943,88 @@
         va[2 * x + 1] = vb[2 * x + 1] + corr
 
     enlarge(X1, lambda x: v1a[GHOST + x, 0:R1, :], inside)
-    for x in range(X1):
-        yrim[0, x : x + 1, :] = v1a[GHOST + x, RE - 1 : RE, :]
-        yrim[1, x : x + 1, :] = v1a[GHOST + x, R1 : R1 + 1, :]
-
-    def rim(k):
-        if k < 2:
-            return v1a[GHOST - 1 if k == 0 else X1 + GHOST, 0:R1, :]
-        if k < 4:
-            return yrim[k - 2]
-        return pltpu.roll(z1a[0:R1, :], LANES - GHOST, 1)
-
-    def outside(k, corr):
-        if k < 2:
-            xh0[k, FIXED] = xh0[k, BLACK] + corr
-        elif k < 4:
-            yh0[k - 2, FIXED] = yh0[k - 2, BLACK] + corr
-        else:
-            zh0[FIXED] = zh0[BLACK] + corr[:, 0:LANES]
-
-    enlarge(5, rim, outside)
+    arrive(5)
+    diagonal = tile_lane == tile_row + GHOST
+    stack, lined_stack = [], []
+    own_pack = jnp.zeros((RE, LANES), F32)
+    for p in range(GHOST, XE - GHOST):
+        own_pack = jnp.where(pack_lane == p, pltpu.roll(v1a[p], p + 1 - iz, 1), own_pack)
+    for k in range(2):
+        p, own = (GHOST - 1, GHOST) if k == 0 else (X1 + GHOST, X1 + GHOST - 1)
+        val, near = near1(lambda p: v1a[p], lambda p: z1a[:, p : p + 1], p, edge=True)
+        stack += [val[0:R1]] + [(other - val)[0:R1] for other in (v1a[own], near[2], near[3])]
+        lined_stack.append(((near[4] - val)[0:R1], (near[5] - val)[0:R1]))
+    for k in range(2):
+        row, own = (RE - 1, 0) if k == 0 else (R1, R1 - 1)
+        for p in range(GHOST - 1, X1 + GHOST + 1):
+            yrim[k, p : p + 1, :] = v1a[p, row : row + 1, :]
+            if GHOST <= p < X1 + GHOST:
+                yrim[2 + k, p : p + 1, :] = v1a[p, own : own + 1, :]
+        val = yrim[k, GHOST : X1 + GHOST, :]
+        others = [
+            yrim[2 + k, GHOST : X1 + GHOST, :],
+            yrim[k, GHOST - 1 : X1 + GHOST - 1, :],
+            yrim[k, GHOST + 1 : X1 + GHOST + 1, :],
+        ]
+        stack += [val] + [other - val for other in others]
+        line = jnp.where(diagonal, jnp.broadcast_to(z1a[row : row + 1, :], (8, LANES)), 0.0)
+        column = jnp.broadcast_to(jnp.sum(line, axis=1, keepdims=True), (8, LANES))
+        back = jnp.where(tile_lane == 0, jnp.where(iz == 0, 0.0, column), pltpu.roll(val, 1, 1))
+        ahead = jnp.where(tile_lane == Z1 - 1, jnp.where(iz == 0, column, 0.0), pltpu.roll(val, Z1 - 1, 1))
+        lined_stack.append((back - val, ahead - val))
+    val = z1a[...]
+    shifts = [pltpu.roll(val, 1, 0), pltpu.roll(val, RE - 1, 0), pltpu.roll(val, 1, 1), pltpu.roll(val, LANES - 1, 1)]
+    face = [val, own_pack - val] + [other - val for other in shifts]
+    face = [pltpu.roll(f[0:R1], LANES - GHOST, 1) for f in face]
+    stack += face[:4]
+    lined_stack.append((face[4], face[5]))
+    for i, piece in enumerate(stack):
+        tall[i * R1 : (i + 1) * R1, 0:Z1] = piece
+    for i, (back, ahead) in enumerate(lined_stack):
+        tall2[i * R1 : (i + 1) * R1, 0:Z1] = back
+        tall2[i * R1 : (i + 1) * R1, Z1 : 2 * Z1] = ahead
+    k = lax.broadcasted_iota(jnp.int32, (2 * Z1, Z0), 0)
+    j = lax.broadcasted_iota(jnp.int32, (2 * Z1, Z0), 1)
+    source = lax.shift_right_logical(j, 1) + Z1 * jnp.bitwise_and(j, 1)
+    big = dot(tall[0 : len(stack) * R1, 0:Z1], double01)
+    lined_big = dot(tall2[0 : len(lined_stack) * R1, :], jnp.where(k == source, 1.0, 0.0).astype(F32))
+
+    def woven(slot, first, second):
+        parts = []
+        for k in range(Z0 // LANES):
+            at = 2 * slot + k
+            tmp[at, pl.ds(0, R1, 2), :] = first[:, k * LANES : (k + 1) * LANES]
+            tmp[at, pl.ds(1, R1, 2), :] = second[:, k * LANES : (k + 1) * LANES]
+            parts.append(tmp[at, 0:R0, :])
+        return jnp.concatenate(parts, axis=1)
+
+    def finished(k):
+        piece = [big[(4 * k + i) * R1 : (4 * k + i + 1) * R1] for i in range(4)]
+        lines = lined_big[k * R1 : (k + 1) * R1]
+        at = 4 * (k % 2)
+        return (
+            woven(at, piece[0], piece[0]),
+            woven(at + 1, piece[1], piece[1]),
+            woven(at + 2, piece[2], piece[3]),
+            woven(at + 3, lines, lines),
+        )
+
+    for k in range(4):
+        ref, side = (xh0, k) if k < 2 else (yh0, k - 2)
+        corr, toward, beside, lengthwise = finished(k)
+        ref[side, FIXED] = ref[side, BLACK] + corr
+        first, second = ref[side, MIXED], ref[side, READY]
+        ref[side, LAST] = ((second + corr) + first * toward) + (
+            pltpu.roll(first, Z0 - 1, 1) * beside + pltpu.roll(second, Z0 - 1, 1) * lengthwise
+        )
+    corr, toward, beside, sideways = [f[:, 0:LANES] for f in finished(4)]
+    zh0[FIXED] = zh0[BLACK] + corr
+    first = zh0[MIXED]
+    zh0[LAST] = ((zh0[READY] + corr) + first * toward) + (
+        pltpu.roll(first, LANES - X0, 1) * sideways + pltpu.roll(first, LANES - 2 * X0, 1) * beside
+    )
     half_sweep(None, halo0, FIXED, va, vb, c0, b0, 0)
-    publish(5, halo0, LAST, vb)
-    half_sweep(5, halo0, LAST, vb, ext_out, c0, b0, 1)
+    half_sweep(None, halo0, LAST, vb, ext_out, c0, b0, 1)
 
     for number in range(len(EXCHANGES)):
         sent(number)
@@ -970,7 +1057,7 @@
         assert R1 == 8 and X1 == 8 and X % 8 == 0
         total = nx * ny * nz
         assert labels.shape == (2, 2, LANES // 4)
-        f0 = 9
+        f0 = 11
         field = (X, R, Z)
         lvl1 = (X1, R1, Z1)
         whole = (XG, RG, ZG)
@@ -989,14 +1076,15 @@
         scratch += [v(*field), v(*field)]
         scratch += [
             v(2 * max(X1, XG // 2), max(R, RG), LANES),
-            v(max(X1 * R1, (XG // 2) * (RG // 2), 2 * X1 * R1, total), Z),
+            v(max(X1 * R1, (XG // 2) * (RG // 2), 2 * X1 * R1, 20 * R1, total), Z),
         ]
         XE, RE = X1 + 2 * GHOST, R1 + 2 * GHOST
         assert GHOST * XE <= LANES and 2 * GHOST == R1 and GHOST <= X1
         wide, pack = (XE, RE, Z1), (RE, LANES)
         scratch += [v(3, *wide), v(2, 3, X1 // 2, R1, Z1), v(2, 3, XE // 2, R1, Z1), v(3, R1, LANES)]
         scratch += [v(9, 3, R1, LANES), v(3, *pack), v(6, *wide), v(6, *pack), v(*lvl1), v(*lvl1)]
-        scratch += [v(*wide), v(*wide), v(*pack), v(*pack), v(2, X1, Z1)]
+        scratch += [v(*wide), v(*wide), v(*pack), v(*pack), v(4, XE, Z1)]
+        scratch += [v(*field), v(8 * R1, Z)]
         scratch += [v(1, LANES), v(total, 1, LANES), v(8, LANES), v(total, 8, LANES), v(8, LANES), v(total, 8, LANES)]
         scratch += [v(*whole), v(*whole), v(6, *whole), v(*whole), v(*whole), v(*whole), v(*whole)]
         scratch += [v(6, *third), v(*third), v(*third)]

time: 41.7 us -> 38.7 us (0.928)
  Pallas kernels: 40.3 us -> 37.2 us
    pallas_call x1, Pallas kernels: 39.3 us -> 36.3 us  [on_device(): pl.pallas_call(functools.partial(kernel, (nx, ny, nz)), out_shape=[shape]...]
where the time goes in v4:
time: 38.7 us; the launch traced here: 38.6 us
  Pallas kernels  37.2 us (96%)
  local copies, waits for them, and re-layouts  0.67 us (2%)
  between operations  0.65 us (2%)
    pallas_call x1, Pallas kernels, on_device(): pl.pallas_call(functools.partial(kernel, (nx, ny, nz)), out_shape=[shape]...  36.3 us
    pallas_call x1, Pallas kernels, on_device(): pl.pallas_call(finish, out_shape=[shape] * 3, in_specs=[vmem] * 3, out_sp...  0.9 us

profile of v4, /device:TPU:0, one launch (start us, length us, event | category | flops | bytes accessed | tf_op | source)
XLA Modules:
  0.0 38.6 jit_solution(10709772337971785952)
XLA Ops:
  0.6 0.0 copy-start
  0.6 0.7 %copy-done = s32[2,2,32]{2,1,0:T(2,128)S(1)} copy-done((s32[2,2,32]{2,1,0:T(2,128)S(1)}, s32[2,2,32]{2,1,0:T(2,128)}, u32[]{:S(2)}) %copy-start) | copy-done | bytes 536
  1.3 36.3 %shard_map.76 = (f32[16,16,256]{2,1,0:T(8,128)S(1)}, f32[16,16,256]{2,1,0:T(8,128)S(1)}, f32[16,16,256]{2,1,0:T(8,128)S(1)}) custom-call(f32[16,16,256]{2,1,0:T(8,128)} %refs_0_.1, f32[16,16,256]{2,1,0:T(8,128)} %refs_1_.1, f32[16,16,256]{2,1,0:T(8,128)} %refs_2_.1, f32[16,16,256]{2,1,0:T(8,128)} %refs_3_.1, s32[2,2,32]{2,1,0:T(2,128)S(1)} %copy-done), custom_call_target="tpu_custom_call" | custom-call | tf_op jit(solution)/shard_map/pallas_call | solution.py:1100
  37.6 0.9 %shard_map.77 = (f32[16,16,256]{2,1,0:T(8,128)}, f32[16,16,256]{2,1,0:T(8,128)}, f32[16,16,256]{2,1,0:T(8,128)}) custom-call(f32[16,16,256]{2,1,0:T(8,128)S(1)} %get-tuple-element.6.refs_0_, f32[16,16,256]{2,1,0:T(8,128)S(1)} %get-tuple-element.7.refs_1_, f32[16,16,256]{2,1,0:T(8,128)S(1)} %get-tuple-element.8.refs_2_), custom_call_target="tpu_custom_call" | custom-call | tf_op jit(solution)/shard_map/pallas_call | solution.py:1111
Async XLA Ops:
  0.6 0.7 %copy-start = (s32[2,2,32]{2,1,0:T(2,128)S(1)}, s32[2,2,32]{2,1,0:T(2,128)}, u32[]{:S(2)}) copy-start(s32[2,2,32]{2,1,0:T(2,128)} %refs_4_.1) | copy-start | bytes 1540

commit v5 on v4

--- a/solution.py
+++ b/solution.py
@@ -22,7 +22,7 @@
 GHOST = 4
 EXCHANGES = (
     (INNER, 2),
-    (OUTER, 2),
+    (V, 1),
     (NEXT, 1),
     (RED, 1),
     (BLACK, 1),
@@ -35,7 +35,15 @@
 
 
 def dot(a, b):
-    return jnp.dot(a, b, precision=lax.Precision.HIGHEST, preferred_element_type=F32)
+    high = a.astype(jnp.bfloat16)
+    rest = a - high.astype(F32)
+    middle = rest.astype(jnp.bfloat16)
+    low = (rest - middle.astype(F32)).astype(jnp.bfloat16)
+    chosen = b.astype(jnp.bfloat16)
+    rows = a.shape[0]
+    both = jnp.dot(jnp.concatenate([low, middle, high], axis=0), chosen, preferred_element_type=F32)
+    parts = [both[i * rows : (i + 1) * rows] for i in range(3)]
+    return (parts[0] + parts[1]) + parts[2]
 
 
 def pair_matrix(rows, cols, offset):
@@ -144,8 +152,8 @@
     (xs0, ys0, zs0, xh0, yh0, zh0) = refs[7:13]
     (in0, out0, uu, w0, c0, d0, b0, va, vb, tmp, tall) = refs[13:24]
     (ee, ys1, yr1, zs1, zr1, zp1, c1, cz1, d1, b1, v1a, v1b, z1a, z1b, yrim, mixed, tall2) = refs[24:41]
-    (lab_own, lab_all, gc_own, gc, gr_own, gr, in2, out2, c2, d2, b2, v2a, v2b) = refs[41:54]
-    (c3, b3, v3, k3, h3, send_sem, recv_sem, wide_send, wide_recv, gs_sem, gr_sem) = refs[54:]
+    (gc_own, gc, gr_own, gr, in2, out2, c2, d2, b2, v2a, v2b) = refs[41:52]
+    (c3, b3, v3, k3, h3, send_sem, recv_sem, wide_send, wide_recv, gs_sem, gr_sem) = refs[52:]
     nx, ny, nz = counts
     ix, iy, iz = lax.axis_index("gx"), lax.axis_index("gy"), lax.axis_index("gz")
     me = (ix * ny + iy) * nz + iz
@@ -161,7 +169,7 @@
     barrier = pltpu.get_barrier_semaphore()
 
     def others(body):
-        for i in range(1, total):
+        for i in sorted(range(1, total), key=lambda i: (abs(i // nz % ny * 2 - ny), i)):
             dev = me + i
             body(jnp.where(dev >= total, dev - total, dev))
 
@@ -392,12 +400,6 @@
             )
         )
 
-    spread = copy_matrix(lab.shape[2], LANES, 0)
-
-    def lab_lane(bx, by, at):
-        line = jnp.dot(lab[bx].astype(F32), spread, preferred_element_type=F32)[by : by + 1]
-        return jnp.broadcast_to(pltpu.roll(jnp.broadcast_to(line, (8, LANES)), at * lab.shape[2], 1), (8, LANES))
-
     def label_of(x):
         return lab_planes[x // 8]
 
@@ -406,18 +408,10 @@
         in0[x] = jnp.where(label == 1.0, 1.0, jnp.where(label == 2.0, 0.3, 0.0)) * fib[x]
         out0[x] = jnp.where(label == 0.0, 3.0, 1.0)
         uu[x] = mem[x] + ext[x]
-    acc = jnp.zeros((8, LANES), F32)
-    for bx in range(lab.shape[0]):
-        for by in range(lab.shape[1]):
-            at = bx * lab.shape[1] + by
-            acc = jnp.where(lax.shift_right_logical(tile_lane, 5) == at, lab_lane(bx, by, at), acc)
-    lab_own[...] = acc[0:1]
     halo0.put(INNER, in0)
     halo0.put(U, uu)
     pl.semaphore_wait(barrier, total - 1)
     send(0)
-    gather_send(lab_own, lab_all, 2)
-    halo0.put(OUTER, out0)
     halo0.put(V, ext)
     send(1)
 
@@ -478,7 +472,11 @@
     even_row = jnp.bitwise_and(g0.row, 1) == 0
     first0 = (g0.lane == 0) & (iz == 0)
     last0 = (g0.lane == Z0 - 1) & (iz == nz - 1)
-    arrive(1)
+    for side in range(2):
+        for ref, has in ((xh0, here), (yh0, along)):
+            val = jnp.where(ref[side, INNER] == 0.0, 3.0, 1.0)
+            ref[side, OUTER] = jnp.where(has[2 * side - 1], val, 0.0)
+    zh0[OUTER] = jnp.where(zh0[INNER] == 0.0, 3.0, 1.0)
     inv0 = vb
     for x in range(X0):
         centre, near = halo0.neighbours(OUTER, lambda x: out0[x], x, edge=True)
@@ -502,6 +500,7 @@
             val, new = update(halo, slot, lambda x: src[x], c, b, x)
             dst[x] = jnp.where(halo.grid.colour(x, colour), new, val)
 
+    arrive(1)
     for x in inner_first(2, X0):
         m, near = halo0.neighbours(NEXT, lambda x: mem_out[x], x)
         rhs = jnp.zeros_like(m)
@@ -575,50 +574,14 @@
         inv = jnp.where(inside, 1.0 / diag, 0.0)
         return [jnp.where(inside, f * inv, 0.0) for f in full], diag, inv
 
-    gather_wait(lab_all, 2, True)
-    blocks = [(sx, bx) for sx, bx in ((-1, 1), (0, 0), (0, 1), (1, 0))]
-    lines = [(0, 0), (0, 1), (1, 0), (-1, 1)]
-    span = lab.shape[2]
-    for z in range(2):
-        core = iz if z == 0 else 1 - iz
-        for i, (sx, bx) in enumerate(blocks):
-            for j, (sy, by) in enumerate(lines):
-                px, py = jnp.clip(ix + sx, 0, nx - 1), jnp.clip(iy + sy, 0, ny - 1)
-                at = (z * 4 + i) * 4 + j
-                tall[at : at + 1, 0:LANES] = lab_all[(px * ny + py) * nz + core]
-    near_labels = tall[0:32, 0:LANES]
-    order = lax.bitwise_and(lax.broadcasted_iota(jnp.int32, (32, LANES), 0), 15)
-    segment = jnp.zeros((32, LANES), jnp.int32)
-    for i, (_, bx) in enumerate(blocks):
-        for j, (_, by) in enumerate(lines):
-            segment = jnp.where(order == i * 4 + j, bx * lab.shape[1] + by, segment)
-    lined = near_labels
-    for k in range(1, LANES // span):
-        lined = jnp.where(segment == k, pltpu.roll(near_labels, LANES - k * span, 1), lined)
-    stretched = jnp.dot(lined[0:16], copy_matrix(LANES, Z1, 2), preferred_element_type=F32)
-    edge_labels = jnp.where(iz == 0, lined[16:32, 0:1], lined[16:32, span - 1 : span])
-    edge_labels = jnp.broadcast_to(edge_labels, (16, LANES))
-    group = lax.shift_right_logical(g1.row, 2)
-    pack_group = lax.shift_right_logical(pack_row, 2)
-    pack_block = lax.shift_right_logical(pack_x, 2)
-    packed_labels = jnp.zeros((RE, LANES), F32)
-    for i in range(4):
-        block_labels = jnp.zeros((RE, Z1), F32)
-        for j in range(4):
-            at = i * 4 + j
-            block_labels = jnp.where(
-                group == j, jnp.broadcast_to(stretched[at : at + 1], (RE, Z1)), block_labels
-            )
-            packed_labels = jnp.where(
-                (pack_group == j) & (pack_block == i),
-                jnp.broadcast_to(edge_labels[at : at + 1], (RE, LANES)),
-                packed_labels,
-            )
-        block_outer = jnp.where(block_labels == 0.0, 3.0, 1.0)
-        for p in range(4 * i, 4 * i + 4):
-            ee[OUTER1, p] = jnp.where(inside1(p), block_outer, 0.0)
-    zp1[OUTER1] = jnp.where(pack_inside, jnp.where(packed_labels == 0.0, 3.0, 1.0), 0.0)
     wide_arrive(0)
+
+    def outer_of(inner):
+        return jnp.where(inner == 0.0, 3.0, 1.0)
+
+    for p in range(XE):
+        ee[OUTER1, p] = jnp.where(inside1(p), outer_of(ee[INNER1, p]), 0.0)
+    zp1[OUTER1] = jnp.where(pack_inside, outer_of(zp1[INNER1]), 0.0)
     for p in range(1, XE - 1):
         ci, ni = near1(lambda p: ee[INNER1, p], lambda p: zp1[INNER1, :, p : p + 1], p, edge=True)
         co, no = near1(lambda p: ee[OUTER1, p], lambda p: zp1[OUTER1, :, p : p + 1], p, edge=True)
@@ -784,26 +747,8 @@
     send(5)
     gather_wait(gc, 0, True)
     unpack(lambda t: gc[t], in2)
-    for t in range(total):
-        tall[t : t + 1, 0:LANES] = lab_all[t]
-    k = lax.broadcasted_iota(jnp.int32, (LANES, LANES), 0)
-    j = lax.broadcasted_iota(jnp.int32, (LANES, LANES), 1)
-    from_lane = lax.div(j, half) * (lab.shape[1] * span) + lax.div(lax.rem(j, half), half // span)
-    every = [
-        jnp.dot(
-            tall[0:total, 0:LANES],
-            jnp.where(k == from_lane + by * span, 1.0, 0.0).astype(F32),
-            preferred_element_type=F32,
-        )
-        for by in range(2)
-    ]
-    first_rows = lax.rem(tile_row, R2) < R2 // 2
-
-    def label_tile(t):
-        pair = [jnp.broadcast_to(e[t : t + 1], (8, LANES)) for e in every]
-        return jnp.where(jnp.where(first_rows, pair[0], pair[1]) == 0.0, 3.0, 1.0)
-
-    unpack(label_tile, out2)
+    for x in range(XG):
+        out2[x] = outer_of(in2[x])
     whole_couplings(g2, in2, out2, ZG - 1, c2, d2, b2)
     for x, val in enumerate(restrict2(lambda x: in2[x], 0.125)):
         v3[x] = val
@@ -824,6 +769,10 @@
             k3[colour * 6 + 1, p] = pack(colour, c3[0, a], c3[1, z])
             for k in range(2, 6):
                 k3[colour * 6 + k, p] = pack(colour, c3[k, a], c3[k, z])
+            if colour == 0:
+                for k in range(6):
+                    k3[12 + k, p] = pltpu.roll(k3[k, p], 1, 1)
+                    k3[18 + k, p] = pltpu.roll(k3[k, p], ZG - 1, 1)
 
     wide_arrive(1)
     ring = GHOST - 1
@@ -844,6 +793,7 @@
     half_pack(v1a, z1a, z1b, 1, 0, XE)
     half1(v1a, z1a, v1b, 1, (1, 2, XE - 3, XE - 2))
     gather_wait(gr, 1, True)
+    arrive(5)
     unpack(lambda t: gr[t], v2b)
     for x in range(XG):
         b2[x] = v2b[x] * b2[x]
@@ -864,24 +814,31 @@
             h3[colour, p] = pack(colour, b3[2 * p], b3[2 * p + 1])
     none = jnp.zeros((RH, ZG), F32)
 
-    def relaxed(colour, other):
+    at_shift = {0: 0, 1: 12, -1: 18}
+    first_h = {s: [pltpu.roll(h3[0, p], s % ZG, 1) if s else h3[0, p] for p in range(XP)] for s in STEPS}
+
+    def relaxed(colour, shift, shifted):
         fresh = []
         for p in range(XP):
-            val, at = other[p], colour * 6
-            before = other[p - 1] if p > 0 else none
-            after = other[p + 1] if p < XP - 1 else none
-            i = h3[colour, p] + k3[at, p] * val
-            j = k3[at + 1, p] * pack(colour, before, after) + k3[at + 2, p] * pltpu.roll(val, 1, 0)
-            l = k3[at + 3, p] * pltpu.roll(val, RH - 1, 0) + k3[at + 4, p] * pltpu.roll(val, 1, 1)
-            fresh.append((i + k3[at + 5, p] * pltpu.roll(val, ZG - 1, 1)) + (j + l))
+            val, at = shifted[shift][p], colour * 6 + at_shift[shift]
+            before = shifted[shift][p - 1] if p > 0 else none
+            after = shifted[shift][p + 1] if p < XP - 1 else none
+            i = (h3[1, p] if colour else first_h[shift][p]) + k3[at, p] * val
+            mask = own[(colour + shift) % 2]
+            j = k3[at + 1, p] * jnp.where(mask, before, after) + k3[at + 2, p] * pltpu.roll(val, 1, 0)
+            l = k3[at + 3, p] * pltpu.roll(val, RH - 1, 0) + k3[at + 4, p] * shifted[shift + 1][p]
+            fresh.append((i + k3[at + 5, p] * shifted[shift - 1][p]) + (j + l))
         return fresh
 
     def coarse(step, state):
-        red = relaxed(0, state[XP:])
-        black = relaxed(1, red)
-        return tuple(red + black)
-
-    state = lax.fori_loop(0, COARSE_SWEEPS, coarse, (none,) * (2 * XP))
+        shifted = {0: state[XP:]}
+        for s in (-2, -1, 1, 2):
+            shifted[s] = [pltpu.roll(v, s % ZG, 1) for v in shifted[0]]
+        red = {s: relaxed(0, s, shifted) for s in STEPS}
+        return tuple(red[0] + relaxed(1, 0, red))
+
+    start = relaxed(1, 0, first_h)
+    state = lax.fori_loop(1, COARSE_SWEEPS, coarse, tuple(first_h[0] + start))
     solved = []
     for p in range(XP):
         solved.append(pack(0, state[p], state[XP + p]))
@@ -943,7 +900,6 @@
         va[2 * x + 1] = vb[2 * x + 1] + corr
 
     enlarge(X1, lambda x: v1a[GHOST + x, 0:R1, :], inside)
-    arrive(5)
     diagonal = tile_lane == tile_row + GHOST
     stack, lined_stack = [], []
     own_pack = jnp.zeros((RE, LANES), F32)
@@ -1032,7 +988,6 @@
         wide_sent(number)
     gather_wait(gc, 0, False)
     gather_wait(gr, 1, False)
-    gather_wait(lab_all, 2, False)
 
 
 def finish(*refs):
@@ -1085,15 +1040,15 @@
         scratch += [v(9, 3, R1, LANES), v(3, *pack), v(6, *wide), v(6, *pack), v(*lvl1), v(*lvl1)]
         scratch += [v(*wide), v(*wide), v(*pack), v(*pack), v(4, XE, Z1)]
         scratch += [v(*field), v(8 * R1, Z)]
-        scratch += [v(1, LANES), v(total, 1, LANES), v(8, LANES), v(total, 8, LANES), v(8, LANES), v(total, 8, LANES)]
+        scratch += [v(8, LANES), v(total, 8, LANES), v(8, LANES), v(total, 8, LANES)]
         scratch += [v(*whole), v(*whole), v(6, *whole), v(*whole), v(*whole), v(*whole), v(*whole)]
         scratch += [v(6, *third), v(*third), v(*third)]
         packed = (XG // 4, RG // 2, ZG)
-        scratch += [v(12, *packed), v(2, *packed)]
+        scratch += [v(24, *packed), v(2, *packed)]
         sems = SIDES * len(EXCHANGES)
         scratch += [pltpu.SemaphoreType.DMA((sems,))] * 2
         scratch += [pltpu.SemaphoreType.DMA((WIDE_SIDES * len(WIDE),))] * 2
-        scratch += [pltpu.SemaphoreType.DMA((3,))] * 2
+        scratch += [pltpu.SemaphoreType.DMA((2,))] * 2
         vmem = pl.BlockSpec(memory_space=pltpu.VMEM)
         room = 54400 << 10
         shape = jax.ShapeDtypeStruct(field, F32)

time: 38.7 us -> 37.4 us (0.966)
  Pallas kernels: 37.2 us -> 35.9 us
    pallas_call x1, Pallas kernels: 36.3 us -> 35 us  [on_device(): pl.pallas_call(functools.partial(kernel, (nx, ny, nz)), out_shape=[shape]...]
where the time goes in v5:
time: 37.4 us; the launch traced here: 37.2 us
  Pallas kernels  35.9 us (96%)
  local copies, waits for them, and re-layouts  0.67 us (2%)
  between operations  0.65 us (2%)
    pallas_call x1, Pallas kernels, on_device(): pl.pallas_call(functools.partial(kernel, (nx, ny, nz)), out_shape=[shape]...  35 us
    pallas_call x1, Pallas kernels, on_device(): pl.pallas_call(finish, out_shape=[shape] * 3, in_specs=[vmem] * 3, out_sp...  0.9 us

profile of v5, /device:TPU:0, one launch (start us, length us, event | category | flops | bytes accessed | tf_op | source)
XLA Modules:
  0.0 37.2 jit_solution(1480043979235884329)
XLA Ops:
  0.6 0.0 copy-start
  0.6 0.7 %copy-done = s32[2,2,32]{2,1,0:T(2,128)S(1)} copy-done((s32[2,2,32]{2,1,0:T(2,128)S(1)}, s32[2,2,32]{2,1,0:T(2,128)}, u32[]{:S(2)}) %copy-start) | copy-done | bytes 536
  1.3 35.0 %shard_map.76 = (f32[16,16,256]{2,1,0:T(8,128)S(1)}, f32[16,16,256]{2,1,0:T(8,128)S(1)}, f32[16,16,256]{2,1,0:T(8,128)S(1)}) custom-call(f32[16,16,256]{2,1,0:T(8,128)} %refs_0_.1, f32[16,16,256]{2,1,0:T(8,128)} %refs_1_.1, f32[16,16,256]{2,1,0:T(8,128)} %refs_2_.1, f32[16,16,256]{2,1,0:T(8,128)} %refs_3_.1, s32[2,2,32]{2,1,0:T(2,128)S(1)} %copy-done), custom_call_target="tpu_custom_call" | custom-call | tf_op jit(solution)/shard_map/pallas_call | solution.py:1055
  36.3 0.9 %shard_map.77 = (f32[16,16,256]{2,1,0:T(8,128)}, f32[16,16,256]{2,1,0:T(8,128)}, f32[16,16,256]{2,1,0:T(8,128)}) custom-call(f32[16,16,256]{2,1,0:T(8,128)S(1)} %get-tuple-element.6.refs_0_, f32[16,16,256]{2,1,0:T(8,128)S(1)} %get-tuple-element.7.refs_1_, f32[16,16,256]{2,1,0:T(8,128)S(1)} %get-tuple-element.8.refs_2_), custom_call_target="tpu_custom_call" | custom-call | tf_op jit(solution)/shard_map/pallas_call | solution.py:1066
Async XLA Ops:
  0.6 0.7 %copy-start = (s32[2,2,32]{2,1,0:T(2,128)S(1)}, s32[2,2,32]{2,1,0:T(2,128)}, u32[]{:S(2)}) copy-start(s32[2,2,32]{2,1,0:T(2,128)} %refs_4_.1) | copy-start | bytes 1540

commit v6 on v5

--- a/solution.py
+++ b/solution.py
@@ -173,7 +173,24 @@
             dev = me + i
             body(jnp.where(dev >= total, dev - total, dev))
 
-    others(lambda dev: pl.semaphore_signal(barrier, inc=1, device_id=dev, device_id_type=LOGICAL))
+    close = nx <= 4 and ny <= 4
+    if close:
+        greeted = -1
+        for dx in (-1, 0, 1):
+            for dy in (-1, 0, 1):
+                present = (ix + dx >= 0) & (ix + dx < nx) & (iy + dy >= 0) & (iy + dy < ny)
+                greeted = greeted + jnp.where(present, nz, 0)
+                for z in (iz, 1 - iz):
+                    if dx == 0 and dy == 0 and z is iz:
+                        continue
+
+                    def hail(where=(ix + dx, iy + dy, z)):
+                        pl.semaphore_signal(barrier, inc=1, device_id=where, device_id_type=MESH)
+
+                    pl.when(present)(hail)
+    else:
+        greeted = total - 1
+        others(lambda dev: pl.semaphore_signal(barrier, inc=1, device_id=dev, device_id_type=LOGICAL))
 
     def clear(missing, ref, side):
         def fill():
@@ -305,6 +322,19 @@
 
     def wide_publish(number):
         first, count = WIDE[number]
+        plan = list(wide_copies(number))
+
+        def start(group):
+            for copy, goes, _ in group:
+                maybe(goes, copy.start)
+
+        start(plan[:2])
+        for slot in range(first, first + count):
+            for k in range(X1 // 2):
+                even, odd = ee[slot, GHOST + 2 * k, 0:R1, :], ee[slot, GHOST + 2 * k + 1, 0:R1, :]
+                ys1[0, slot, k] = jnp.where(tile_row < GHOST, even, pltpu.roll(odd, GHOST, 0))
+                ys1[1, slot, k] = jnp.where(tile_row < GHOST, pltpu.roll(odd, GHOST, 0), even)
+        start(plan[2:8])
         for slot in range(first, first + count):
             acc = jnp.zeros((R1, LANES), F32)
             for x in range(X1):
@@ -314,12 +344,7 @@
                     shift = jnp.where(iz == 0, at + 1 + depth, at - depth)
                     acc = jnp.where(tile_lane == at, pltpu.roll(val, shift, 1), acc)
             zs1[slot] = acc
-            for k in range(X1 // 2):
-                even, odd = ee[slot, GHOST + 2 * k, 0:R1, :], ee[slot, GHOST + 2 * k + 1, 0:R1, :]
-                ys1[0, slot, k] = jnp.where(tile_row < GHOST, even, pltpu.roll(odd, GHOST, 0))
-                ys1[1, slot, k] = jnp.where(tile_row < GHOST, pltpu.roll(odd, GHOST, 0), even)
-        for copy, goes, _ in wide_copies(number):
-            maybe(goes, copy.start)
+        start(plan[8:])
 
     def keep(condition, val):
         return val if condition is None else jnp.where(condition, val, 0.0)
@@ -408,10 +433,13 @@
         in0[x] = jnp.where(label == 1.0, 1.0, jnp.where(label == 2.0, 0.3, 0.0)) * fib[x]
         out0[x] = jnp.where(label == 0.0, 3.0, 1.0)
         uu[x] = mem[x] + ext[x]
-    halo0.put(INNER, in0)
-    halo0.put(U, uu)
-    pl.semaphore_wait(barrier, total - 1)
-    send(0)
+    halo0.put_ends(INNER, in0)
+    halo0.put_ends(U, uu)
+    pl.semaphore_wait(barrier, greeted)
+    send(0, ends)
+    halo0.put_rest(INNER, in0)
+    halo0.put_rest(U, uu)
+    send(0, rest)
     halo0.put(V, ext)
     send(1)
 
@@ -510,7 +538,6 @@
         val, new = update(halo0, V, lambda x: ext[x], c0, b0, x)
         va[x] = jnp.where(g0.colour(x, 0), new, val)
     publish(3, halo0, RED, va)
-    gather_send(gc_own, gc, 0)
 
     first1 = (g1.lane == 0) & (iz == 0)
     last1 = (g1.lane == Z1 - 1) & (iz == nz - 1)
@@ -745,6 +772,25 @@
     wide_publish(1)
     halo0.put(READY, mixed)
     send(5)
+    gather_send(gc_own, gc, 0)
+    wide_arrive(1)
+    ring = GHOST - 1
+    for p in range(ring - 1, XE - ring + 1):
+        v1a[p] = jnp.where(g1.colour(p, 0), ee[RHS1, p], 0.0)
+    z1a[...] = jnp.where(pack_own[0], zp1[RHS1], 0.0)
+    half_pack(v1a, z1a, z1b, 1, ring, XE - ring)
+    half1(v1a, z1a, v1b, 1, range(ring, XE - ring))
+
+    def residual1(x):
+        val, new = update1(v1b, z1b, GHOST + x)
+        return d1[x] * (new - val)[0:R1]
+
+    gr_own[...] = restrict1(residual1, 0.5)
+    gather_send(gr_own, gr, 1)
+    for p in (0, 1, XE - 2, XE - 1):
+        v1a[p] = jnp.where(g1.colour(p, 0), ee[RHS1, p], 0.0)
+    half_pack(v1a, z1a, z1b, 1, 0, XE)
+    half1(v1a, z1a, v1b, 1, (1, 2, XE - 3, XE - 2))
     gather_wait(gc, 0, True)
     unpack(lambda t: gc[t], in2)
     for x in range(XG):
@@ -774,24 +820,6 @@
                     k3[12 + k, p] = pltpu.roll(k3[k, p], 1, 1)
                     k3[18 + k, p] = pltpu.roll(k3[k, p], ZG - 1, 1)
 
-    wide_arrive(1)
-    ring = GHOST - 1
-    for p in range(ring - 1, XE - ring + 1):
-        v1a[p] = jnp.where(g1.colour(p, 0), ee[RHS1, p], 0.0)
-    z1a[...] = jnp.where(pack_own[0], zp1[RHS1], 0.0)
-    half_pack(v1a, z1a, z1b, 1, ring, XE - ring)
-    half1(v1a, z1a, v1b, 1, range(ring, XE - ring))
-
-    def residual1(x):
-        val, new = update1(v1b, z1b, GHOST + x)
-        return d1[x] * (new - val)[0:R1]
-
-    gr_own[...] = restrict1(residual1, 0.5)
-    gather_send(gr_own, gr, 1)
-    for p in (0, 1, XE - 2, XE - 1):
-        v1a[p] = jnp.where(g1.colour(p, 0), ee[RHS1, p], 0.0)
-    half_pack(v1a, z1a, z1b, 1, 0, XE)
-    half1(v1a, z1a, v1b, 1, (1, 2, XE - 3, XE - 2))
     gather_wait(gr, 1, True)
     arrive(5)
     unpack(lambda t: gr[t], v2b)

time: 37.4 us -> 36.6 us (0.979)
  Pallas kernels: 35.9 us -> 35.1 us
    pallas_call x1, Pallas kernels: 35 us -> 34.2 us  [on_device(): pl.pallas_call(functools.partial(kernel, (nx, ny, nz)), out_shape=[shape]...]
where the time goes in v6:
time: 36.6 us; the launch traced here: 36.4 us
  Pallas kernels  35.1 us (96%)
  local copies, waits for them, and re-layouts  0.67 us (2%)
  between operations  0.65 us (2%)
    pallas_call x1, Pallas kernels, on_device(): pl.pallas_call(functools.partial(kernel, (nx, ny, nz)), out_shape=[shape]...  34.2 us
    pallas_call x1, Pallas kernels, on_device(): pl.pallas_call(finish, out_shape=[shape] * 3, in_specs=[vmem] * 3, out_sp...  0.9 us

profile of v6, /device:TPU:0, one launch (start us, length us, event | category | flops | bytes accessed | tf_op | source)
XLA Modules:
  0.0 36.4 jit_solution(13143009951088224907)
XLA Ops:
  0.6 0.0 copy-start
  0.6 0.7 %copy-done = s32[2,2,32]{2,1,0:T(2,128)S(1)} copy-done((s32[2,2,32]{2,1,0:T(2,128)S(1)}, s32[2,2,32]{2,1,0:T(2,128)}, u32[]{:S(2)}) %copy-start) | copy-done | bytes 536
  1.3 34.2 %shard_map.76 = (f32[16,16,256]{2,1,0:T(8,128)S(1)}, f32[16,16,256]{2,1,0:T(8,128)S(1)}, f32[16,16,256]{2,1,0:T(8,128)S(1)}) custom-call(f32[16,16,256]{2,1,0:T(8,128)} %refs_0_.1, f32[16,16,256]{2,1,0:T(8,128)} %refs_1_.1, f32[16,16,256]{2,1,0:T(8,128)} %refs_2_.1, f32[16,16,256]{2,1,0:T(8,128)} %refs_3_.1, s32[2,2,32]{2,1,0:T(2,128)S(1)} %copy-done), custom_call_target="tpu_custom_call" | custom-call | tf_op jit(solution)/shard_map/pallas_call | solution.py:1083
  35.5 0.9 %shard_map.77 = (f32[16,16,256]{2,1,0:T(8,128)}, f32[16,16,256]{2,1,0:T(8,128)}, f32[16,16,256]{2,1,0:T(8,128)}) custom-call(f32[16,16,256]{2,1,0:T(8,128)S(1)} %get-tuple-element.6.refs_0_, f32[16,16,256]{2,1,0:T(8,128)S(1)} %get-tuple-element.7.refs_1_, f32[16,16,256]{2,1,0:T(8,128)S(1)} %get-tuple-element.8.refs_2_), custom_call_target="tpu_custom_call" | custom-call | tf_op jit(solution)/shard_map/pallas_call | solution.py:1094
Async XLA Ops:
  0.6 0.7 %copy-start = (s32[2,2,32]{2,1,0:T(2,128)S(1)}, s32[2,2,32]{2,1,0:T(2,128)}, u32[]{:S(2)}) copy-start(s32[2,2,32]{2,1,0:T(2,128)} %refs_4_.1) | copy-start | bytes 1540

commit v7 on v6

--- a/solution.py
+++ b/solution.py
@@ -866,7 +866,9 @@
         return tuple(red[0] + relaxed(1, 0, red))
 
     start = relaxed(1, 0, first_h)
-    state = lax.fori_loop(1, COARSE_SWEEPS, coarse, tuple(first_h[0] + start))
+    state = tuple(first_h[0] + start)
+    for step in range(1, COARSE_SWEEPS):
+        state = coarse(step, state)
     solved = []
     for p in range(XP):
         solved.append(pack(0, state[p], state[XP + p]))

time: 36.6 us -> 36.5 us (level)
  no operation moved by 1% of the time
where the time goes in v7:
time: 36.5 us; the launch traced here: 36.3 us
  Pallas kernels  35 us (96%)
  local copies, waits for them, and re-layouts  0.67 us (2%)
  between operations  0.65 us (2%)
    pallas_call x1, Pallas kernels, on_device(): pl.pallas_call(functools.partial(kernel, (nx, ny, nz)), out_shape=[shape]...  34.1 us
    pallas_call x1, Pallas kernels, on_device(): pl.pallas_call(finish, out_shape=[shape] * 3, in_specs=[vmem] * 3, out_sp...  0.9 us

profile of v7, /device:TPU:0, one launch (start us, length us, event | category | flops | bytes accessed | tf_op | source)
XLA Modules:
  0.0 36.3 jit_solution(17384708259934815398)
XLA Ops:
  0.6 0.0 copy-start
  0.6 0.7 %copy-done = s32[2,2,32]{2,1,0:T(2,128)S(1)} copy-done((s32[2,2,32]{2,1,0:T(2,128)S(1)}, s32[2,2,32]{2,1,0:T(2,128)}, u32[]{:S(2)}) %copy-start) | copy-done | bytes 536
  1.3 34.1 %shard_map.76 = (f32[16,16,256]{2,1,0:T(8,128)S(1)}, f32[16,16,256]{2,1,0:T(8,128)S(1)}, f32[16,16,256]{2,1,0:T(8,128)S(1)}) custom-call(f32[16,16,256]{2,1,0:T(8,128)} %refs_0_.1, f32[16,16,256]{2,1,0:T(8,128)} %refs_1_.1, f32[16,16,256]{2,1,0:T(8,128)} %refs_2_.1, f32[16,16,256]{2,1,0:T(8,128)} %refs_3_.1, s32[2,2,32]{2,1,0:T(2,128)S(1)} %copy-done), custom_call_target="tpu_custom_call" | custom-call | tf_op jit(solution)/shard_map/pallas_call | solution.py:1085
  35.4 0.9 %shard_map.77 = (f32[16,16,256]{2,1,0:T(8,128)}, f32[16,16,256]{2,1,0:T(8,128)}, f32[16,16,256]{2,1,0:T(8,128)}) custom-call(f32[16,16,256]{2,1,0:T(8,128)S(1)} %get-tuple-element.6.refs_0_, f32[16,16,256]{2,1,0:T(8,128)S(1)} %get-tuple-element.7.refs_1_, f32[16,16,256]{2,1,0:T(8,128)S(1)} %get-tuple-element.8.refs_2_), custom_call_target="tpu_custom_call" | custom-call | tf_op jit(solution)/shard_map/pallas_call | solution.py:1096
Async XLA Ops:
  0.6 0.7 %copy-start = (s32[2,2,32]{2,1,0:T(2,128)S(1)}, s32[2,2,32]{2,1,0:T(2,128)}, u32[]{:S(2)}) copy-start(s32[2,2,32]{2,1,0:T(2,128)} %refs_4_.1) | copy-start | bytes 1540
